TPU v7x, 32 devices: a whole 2x2x4 slice. The times are simulated.
32 devices in a mesh: gx: 4 (over z), gy: 8 (over y, x, core).
Axes of the slice: x: 2, y: 2, z: 4, core: 2. Of those that a mesh axis runs over, the one named last changes fastest.
Arguments:
- radiance: bfloat16 [2048, 16, 128], P(('gx', 'gy')), may hold values from 0.049804688 to 2
- emission: float32 [2048, 16, 128], P(('gx', 'gy')), may hold values from 0.01 to 1
- reflectance: float32 [2048, 16, 128], P(('gx', 'gy')), may hold values from 0.1 to 0.9
- patch_area: float32 [2048, 128], P(('gx', 'gy')), may hold values from 0.25 to 4
- form_factor: bfloat16 [4096, 128, 128], P(('gx', 'gy')), may hold values from 0.00049972534 to 0.014953613
- source_index: int32 [32, 128], P(('gx', 'gy')), may hold values from 0 to 63
- target_index: int32 [32, 128], P(('gx', 'gy')), may hold values from 0 to 63
- block_index: int32 [32, 128], P(('gx', 'gy')), may hold values from 0 to 127, each once within a row
- valid_count: int32 [32, 32], P(('gx', 'gy')), may hold values from 0 to 4, as said below
Outputs:
- new_radiance: float32 [2048, 16, 128], P(('gx', 'gy'))
Inputs may be any that keep to these rules, and one draw needn't show every extreme that they name: `valid_count`: entry [d, p] is the number of live slots among the 4 slots of device d toward peer p, the live ones first; every row has an entry equal to 4. `block_index`: each row is a permutation of 0 to 127.
All inputs are finite; a program needn't handle non-finite values.
Results may differ from a plain program's by a relative error of at most 0.0012.
Values may be sent and summed in bfloat16 or wider, within the bound.
A program may use at most 128 MiB of HBM per device.

v0:
```python
import functools

import jax
import jax.numpy as jnp
from jax import lax
from jax.experimental import pallas as pl
from jax.experimental.pallas import tpu as pltpu
from jax.sharding import PartitionSpec as P

MESH = pl.DeviceIdType.MESH
GROUP = 4
LANES = 128
EXCHANGE_MIB = 60
COMBINE_MIB = 60
F32 = jnp.float32
BF16 = jnp.bfloat16


def exchange(
    n,
    inner,
    block_hbm,
    target_hbm,
    count_hbm,
    source_hbm,
    rad_hbm,
    area_hbm,
    form_hbm,
    fwd_hbm,
    arrived_hbm,
    asked_hbm,
    block_ref,
    target_ref,
    count_ref,
    source_ref,
    rad_ref,
    area_ref,
    form_ref,
    weighted_ref,
    bwd_ref,
    served_ref,
    fetched_ref,
    fwd_ref,
    asked_vmem,
    asked_ref,
    form_sem,
    in_sem,
    out_sem,
    send_sems,
    idx_sem,
    bwd_sem,
    rad_sem,
):
    me = lax.axis_index("gx") * inner + lax.axis_index("gy")
    links = block_ref.shape[1]
    slots = links // n
    clusters = rad_ref.shape[0]
    parts = form_sem.shape[0]
    step = links // parts

    def coords(p):
        return (p // inner, p % inner)

    loads = [
        pltpu.make_async_copy(src, dst, in_sem.at[i])
        for i, (src, dst) in enumerate(
            (
                (rad_hbm, rad_ref),
                (area_hbm, area_ref),
                (block_hbm, block_ref),
                (target_hbm, target_ref),
                (count_hbm, count_ref),
                (source_hbm, source_ref),
            )
        )
    ]
    forms = [
        pltpu.make_async_copy(
            form_hbm.at[pl.ds(i * step, step)], form_ref.at[pl.ds(i * step, step)], form_sem.at[i]
        )
        for i in range(parts)
    ]
    for load in loads + forms:
        load.start()

    barrier = pltpu.get_barrier_semaphore()

    def greet(k, c):
        pl.semaphore_signal(
            barrier, inc=1, device_id=coords((me + k) % n), device_id_type=MESH
        )
        return c

    lax.fori_loop(1, n, greet, 0)

    for load in loads:
        load.wait()

    def weigh(c, carry):
        area = area_ref[pl.ds(c, 1), :]
        weighted_ref[c] = (area * rad_ref[c].astype(F32)).astype(BF16)
        return carry

    lax.fori_loop(0, clusters, weigh, 0, unroll=8)

    width = asked_vmem.shape[2]

    def lane_base(p):
        if links == width:
            return 0
        return pl.multiple_of(p * slots // width * width, width)

    def idx_copy(k):
        p = (me + k) % n
        return pltpu.make_async_remote_copy(
            src_ref=source_ref.at[:, pl.ds(lane_base(p), width)],
            dst_ref=asked_vmem.at[me],
            send_sem=send_sems.at[0],
            recv_sem=idx_sem.at[k],
            device_id=coords(p),
            device_id_type=MESH,
        )

    def bwd_copy(k):
        p = (me + k) % n
        return pltpu.make_async_remote_copy(
            src_ref=bwd_ref.at[pl.ds(p * slots, slots)],
            dst_ref=arrived_hbm.at[pl.ds(me * slots, slots)],
            send_sem=send_sems.at[1],
            recv_sem=bwd_sem.at[k],
            device_id=coords(p),
            device_id_type=MESH,
        )

    def rad_copy(k):
        p = (me + k) % n
        return pltpu.make_async_remote_copy(
            src_ref=served_ref.at[pl.ds(p * slots, slots)],
            dst_ref=fetched_ref.at[pl.ds(me * slots, slots)],
            send_sem=send_sems.at[2],
            recv_sem=rad_sem.at[k],
            device_id=coords(p),
            device_id_type=MESH,
        )

    def live_of(p, s):
        return jnp.where(s < count_ref[0, p], 1.0, 0.0).astype(F32)

    for form in forms:
        form.wait()

    def back(t):
        for u in range(GROUP):
            p = (me + 1 + t * GROUP + u) % n
            for s in range(slots):
                l = p * slots + s
                form = form_ref[block_ref[0, l]]
                seen = weighted_ref[target_ref[0, l]]
                got = jnp.dot(seen, form, preferred_element_type=F32)
                bwd_ref[l] = (got * live_of(p, s)).astype(BF16)

    def back_only(t, c):
        back(t)
        return c

    def send_bwd(k, c):
        bwd_copy(k).start()
        return c

    def back_send(t, c):
        back(t)
        for u in range(GROUP):
            k = 1 + t * GROUP + u

            @pl.when(k != n)
            def _():
                bwd_copy(k).start()

        return c

    early = n // GROUP // 2
    lax.fori_loop(0, early, back_only, 0)
    pl.semaphore_wait(barrier, n - 1)

    def send_idx(k, c):
        idx_copy(k).start()
        return c

    lax.fori_loop(1, n, send_idx, 0)
    lax.fori_loop(1, 1 + early * GROUP, send_bwd, 0)
    asked_vmem[me] = source_ref[:, pl.ds(lane_base(me), width)]
    lax.fori_loop(early, n // GROUP, back_send, 0)

    own = pl.ds(me * slots, slots)
    keep_own = pltpu.make_async_copy(bwd_ref.at[own], arrived_hbm.at[own], out_sem.at[0])
    keep_own.start()

    def wait_idx(k, c):
        idx_copy(k).wait_recv()
        return c

    lax.fori_loop(1, n, wait_idx, 0)
    to_smem = pltpu.make_async_copy(asked_vmem, asked_ref, out_sem.at[1])
    to_smem.start()
    to_smem.wait()
    base = me * slots % width

    def serve(k, c):
        p = (me + k) % n
        for s in range(slots):
            served_ref[p * slots + s] = rad_ref[asked_ref[p, 0, base + s]]

        @pl.when(k != n)
        def _():
            rad_copy(k).start()

        return c

    lax.fori_loop(1, n + 1, serve, 0)
    for s in range(slots):
        fetched_ref[me * slots + s] = served_ref[me * slots + s]
    keep_asked = pltpu.make_async_copy(asked_vmem, asked_hbm, out_sem.at[1])
    keep_asked.start()

    def fwd_copy(k):
        mine = pl.ds((me + n - k) % n * slots, slots)
        return pltpu.make_async_copy(fwd_ref.at[mine], fwd_hbm.at[mine], out_sem.at[2])

    def forward(t, c):
        for u in range(GROUP):
            k = t * GROUP + u

            @pl.when(k != 0)
            def _():
                rad_copy(k).wait_recv()

        for u in range(GROUP):
            p = (me + n - t * GROUP - u) % n
            for s in range(slots):
                l = p * slots + s
                form = form_ref[block_ref[0, l]]
                got = lax.dot_general(
                    fetched_ref[l], form, (((1,), (1,)), ((), ())), preferred_element_type=F32
                )
                fwd_ref[l] = got * live_of(p, s)
        for u in range(GROUP):
            fwd_copy(t * GROUP + u).start()
        return c

    lax.fori_loop(0, n // GROUP, forward, 0)

    def wait_bwd(k, c):
        bwd_copy(k).wait_recv()
        return c

    lax.fori_loop(1, n, wait_bwd, 0)
    most = pl.ds(0, (n - 1) * slots)
    for buf, which in ((bwd_ref, 1), (served_ref, 2)):
        pltpu.make_async_copy(buf.at[most], buf.at[most], send_sems.at[which]).wait()
    rows = asked_vmem.at[pl.ds(0, n - 1)]
    pltpu.make_async_copy(rows, rows, send_sems.at[0]).wait()
    keep_own.wait()
    keep_asked.wait()
    pltpu.make_async_copy(fwd_ref, fwd_hbm, out_sem.at[2]).wait()


def combine(
    n,
    inner,
    target_hbm,
    asked_hbm,
    fwd_hbm,
    arrived_hbm,
    em_hbm,
    refl_hbm,
    area_hbm,
    out_hbm,
    em_ref,
    refl_ref,
    area_ref,
    target_ref,
    asked_ref,
    fwd_ref,
    arrived_ref,
    gath,
    ret,
    out_ref,
    in_sem,
    out_sem,
):
    me = lax.axis_index("gx") * inner + lax.axis_index("gy")
    clusters = em_ref.shape[0]
    links = fwd_ref.shape[0]
    slots = links // n
    width = asked_ref.shape[2]
    base = me * slots % width
    parts = out_sem.shape[0]
    step = clusters // parts
    loads = [
        pltpu.make_async_copy(src, dst, in_sem.at[i])
        for i, (src, dst) in enumerate(
            (
                (fwd_hbm, fwd_ref),
                (arrived_hbm, arrived_ref),
                (target_hbm, target_ref),
                (asked_hbm, asked_ref),
                (em_hbm, em_ref),
                (refl_hbm, refl_ref),
                (area_hbm, area_ref),
            )
        )
    ]
    for load in loads:
        load.start()

    def clear(c, carry):
        gath[c] = jnp.zeros(gath.shape[1:], F32)
        ret[c] = jnp.zeros(ret.shape[1:], F32)
        return carry

    lax.fori_loop(0, clusters, clear, 0, unroll=8)
    for load in loads[:4]:
        load.wait()

    def scatter(p, carry):
        for s in range(slots):
            l = p * slots + s
            t = target_ref[0, l]
            c = asked_ref[p, 0, base + s]
            gath[t] += fwd_ref[l]
            ret[c] += arrived_ref[l].astype(F32)
        return carry

    lax.fori_loop(0, n, scatter, 0, unroll=2)

    def finish(c, carry):
        area = area_ref[pl.ds(c, 1), :]
        out_ref[c] = em_ref[c] + refl_ref[c] * (gath[c] + ret[c] / area)
        return carry

    for load in loads[4:]:
        load.wait()
    stores = []
    for i in range(parts):
        lax.fori_loop(i * step, (i + 1) * step, finish, 0, unroll=8)
        rows = pl.ds(i * step, step)
        stores.append(pltpu.make_async_copy(out_ref.at[rows], out_hbm.at[rows], out_sem.at[i]))
        stores[-1].start()
    for store in stores:
        store.wait()


def solution(mesh):
    outer, inner = mesh.shape["gx"], mesh.shape["gy"]
    n = outer * inner

    def shards(
        radiance,
        emission,
        reflectance,
        patch_area,
        form_factor,
        source_index,
        target_index,
        block_index,
        valid_count,
    ):
        clusters, bands, patches = radiance.shape
        links = source_index.shape[1]
        slots = links // n
        tile = (bands, patches)
        hbm = pl.BlockSpec(memory_space=pl.ANY)
        width = min(links, LANES)
        parts = 4
        fwd, arrived, asked = pl.pallas_call(
            functools.partial(exchange, n, inner),
            out_shape=(
                jax.ShapeDtypeStruct((links,) + tile, F32),
                jax.ShapeDtypeStruct((links,) + tile, BF16),
                jax.ShapeDtypeStruct((n, 1, width), jnp.int32),
            ),
            in_specs=[hbm] * 7,
            out_specs=(hbm, hbm, hbm),
            scratch_shapes=[
                pltpu.SMEM(block_index.shape, jnp.int32),
                pltpu.SMEM(target_index.shape, jnp.int32),
                pltpu.SMEM(valid_count.shape, jnp.int32),
                pltpu.VMEM(source_index.shape, jnp.int32),
                pltpu.VMEM(radiance.shape, BF16),
                pltpu.VMEM(patch_area.shape, F32),
                pltpu.VMEM(form_factor.shape, BF16),
                pltpu.VMEM((clusters,) + tile, BF16),
                pltpu.VMEM((links,) + tile, BF16),
                pltpu.VMEM((links,) + tile, BF16),
                pltpu.VMEM((links,) + tile, BF16),
                pltpu.VMEM((links,) + tile, F32),
                pltpu.VMEM((n, 1, width), jnp.int32),
                pltpu.SMEM((n, 1, width), jnp.int32),
                pltpu.SemaphoreType.DMA((parts,)),
                pltpu.SemaphoreType.DMA((6,)),
                pltpu.SemaphoreType.DMA((3,)),
                pltpu.SemaphoreType.DMA((3,)),
                pltpu.SemaphoreType.DMA((n,)),
                pltpu.SemaphoreType.DMA((n,)),
                pltpu.SemaphoreType.DMA((n,)),
            ],
            compiler_params=pltpu.CompilerParams(
                collective_id=0, has_side_effects=True, vmem_limit_bytes=EXCHANGE_MIB * 1024 * 1024
            ),
            name="exchange",
        )(
            block_index,
            target_index,
            valid_count,
            source_index,
            radiance,
            patch_area,
            form_factor,
        )
        return pl.pallas_call(
            functools.partial(combine, n, inner),
            out_shape=jax.ShapeDtypeStruct((clusters,) + tile, F32),
            in_specs=[hbm] * 7,
            out_specs=hbm,
            scratch_shapes=[
                pltpu.VMEM((clusters,) + tile, F32),
                pltpu.VMEM((clusters,) + tile, F32),
                pltpu.VMEM(patch_area.shape, F32),
                pltpu.SMEM(target_index.shape, jnp.int32),
                pltpu.SMEM((n, 1, width), jnp.int32),
                pltpu.VMEM((links,) + tile, F32),
                pltpu.VMEM((links,) + tile, BF16),
                pltpu.VMEM((clusters,) + tile, F32),
                pltpu.VMEM((clusters,) + tile, F32),
                pltpu.VMEM((clusters,) + tile, F32),
                pltpu.SemaphoreType.DMA((7,)),
                pltpu.SemaphoreType.DMA((4,)),
            ],
            compiler_params=pltpu.CompilerParams(vmem_limit_bytes=COMBINE_MIB * 1024 * 1024),
            name="combine",
        )(target_index, asked, fwd, arrived, emission, reflectance, patch_area)

    spec3 = P(("gx", "gy"), None, None)
    spec2 = P(("gx", "gy"), None)
    return jax.shard_map(
        shards,
        mesh=mesh,
        in_specs=(spec3, spec3, spec3, spec2, spec3, spec2, spec2, spec2, spec2),
        out_specs=spec3,
        check_vma=False,
    )
```

profile of v0, /device:TPU:1, one launch (start us, length us, event | category | flops | bytes accessed | tf_op | source)
XLA Modules:
  0.0 35.5 jit_solution(16836066432851325502)
XLA Ops:
  0.0 32.5 %exchange.1 = (f32[128,16,128]{2,1,0:T(8,128)}, bf16[128,16,128]{2,1,0:T(8,128)(2,1)}, s32[32,1,128]{2,1,0:T(1,128)}) custom-call(s32[1,128]{1,0:T(1,128)} %block_hbm.1, s32[1,128]{1,0:T(1,128)} %target_hbm.3, s32[1,32]{1,0:T(1,128)} %count_hbm.1, s32[1,128]{1,0:T(1,128)} %source_hbm.1, bf16[64,16,128]{2,1,0:T(8,128)(2,1)} %rad_hbm.1, f32[64,128]{1,0:T(8,128)} %area_hbm.3, ...), custom_call_target="tpu_custom_call" | custom-call | tf_op jit(solution)/shard_map/exchange/pallas_call | solution.py:375
  32.5 2.9 %combine.1 = f32[64,16,128]{2,1,0:T(8,128)} custom-call(s32[1,128]{1,0:T(1,128)} %target_hbm.3, s32[32,1,128]{2,1,0:T(1,128)} %get-tuple-element.8.asked_hbm, f32[128,16,128]{2,1,0:T(8,128)} %get-tuple-element.9.fwd_hbm, bf16[128,16,128]{2,1,0:T(8,128)(2,1)} %get-tuple-element.10.arrived_hbm, f32[64,16,128]{2,1,0:T(8,128)} %em_hbm.1, ...), custom_call_target="tpu_custom_call" | custom-call | tf_op jit(solution)/shard_map/combine/pallas_call | solution.py:420
where the time goes:
time: 35.9 us; the launch traced here: 35.5 us
  Pallas kernels  35.5 us (99%)
    pallas_call x1, Pallas kernels, shards(): pl.pallas_call(functools.partial(exchange, n, inner), out_shape=(jax.Shap...  32.5 us
    pallas_call x1, Pallas kernels, shards(): pl.pallas_call(functools.partial(combine, n, inner), out_shape=jax.ShapeD...  2.93 us

commit v1 on v0

--- a/solution.py
+++ b/solution.py
@@ -9,7 +9,6 @@
 
 MESH = pl.DeviceIdType.MESH
 GROUP = 4
-LANES = 128
 EXCHANGE_MIB = 60
 COMBINE_MIB = 60
 F32 = jnp.float32
@@ -17,7 +16,7 @@
 
 
 def exchange(
-    n,
+    outer,
     inner,
     block_hbm,
     target_hbm,
@@ -36,6 +35,7 @@
     rad_ref,
     area_ref,
     form_ref,
+    mirrored_ref,
     weighted_ref,
     bwd_ref,
     served_ref,
@@ -47,11 +47,20 @@
     in_sem,
     out_sem,
     send_sems,
+    ready_sem,
+    mirror_sem,
     idx_sem,
     bwd_sem,
     rad_sem,
 ):
-    me = lax.axis_index("gx") * inner + lax.axis_index("gy")
+    n = outer * inner
+    half = n // 2
+    gx, gy = lax.axis_index("gx"), lax.axis_index("gy")
+    me = gx * inner + gy
+    mine = me % half
+    near = me // half * half
+    far = half - near
+    mirror = (outer - 1 - gx) * inner + gy
     links = block_ref.shape[1]
     slots = links // n
     clusters = rad_ref.shape[0]
@@ -61,16 +70,25 @@
     def coords(p):
         return (p // inner, p % inner)
 
+    def mirror_of(p):
+        return (outer - 1 - p // inner) * inner + p % inner
+
+    def peer(k):
+        return jnp.where(k < half, near, far) + (mine + k) % half
+
+    def origin(k):
+        return jnp.where(k < half, near, far) + (mine + n - k) % half
+
     loads = [
         pltpu.make_async_copy(src, dst, in_sem.at[i])
         for i, (src, dst) in enumerate(
             (
                 (rad_hbm, rad_ref),
+                (source_hbm, source_ref),
                 (area_hbm, area_ref),
                 (block_hbm, block_ref),
                 (target_hbm, target_ref),
                 (count_hbm, count_ref),
-                (source_hbm, source_ref),
             )
         )
     ]
@@ -84,16 +102,68 @@
         load.start()
 
     barrier = pltpu.get_barrier_semaphore()
+    pl.semaphore_signal(barrier, inc=1, device_id=coords(mirror), device_id_type=MESH)
 
     def greet(k, c):
-        pl.semaphore_signal(
-            barrier, inc=1, device_id=coords((me + k) % n), device_id_type=MESH
-        )
-        return c
-
-    lax.fori_loop(1, n, greet, 0)
-
-    for load in loads:
+        pl.semaphore_signal(barrier, inc=1, device_id=coords(peer(k)), device_id_type=MESH)
+        return c
+
+    lax.fori_loop(1, half, greet, 0)
+
+    def idx_copy(k):
+        return pltpu.make_async_remote_copy(
+            src_ref=source_ref,
+            dst_ref=asked_vmem.at[me],
+            send_sem=send_sems.at[0],
+            recv_sem=idx_sem.at[k],
+            device_id=coords(peer(k)),
+            device_id_type=MESH,
+        )
+
+    def bwd_copy(k):
+        return pltpu.make_async_remote_copy(
+            src_ref=bwd_ref.at[pl.ds(peer(k) * slots, slots)],
+            dst_ref=arrived_hbm.at[pl.ds(me * slots, slots)],
+            send_sem=send_sems.at[1],
+            recv_sem=bwd_sem.at[k],
+            device_id=coords(peer(k)),
+            device_id_type=MESH,
+        )
+
+    def rad_copy(k):
+        owner = jnp.where(k < half, me, mirror)
+        return pltpu.make_async_remote_copy(
+            src_ref=served_ref.at[pl.ds(k * slots, slots)],
+            dst_ref=fetched_ref.at[pl.ds(owner * slots, slots)],
+            send_sem=send_sems.at[2],
+            recv_sem=rad_sem.at[k],
+            device_id=coords(near + (mine + k) % half),
+            device_id_type=MESH,
+        )
+
+    across = pltpu.make_async_remote_copy(
+        src_ref=rad_ref,
+        dst_ref=mirrored_ref,
+        send_sem=mirror_sem.at[0],
+        recv_sem=mirror_sem.at[1],
+        device_id=coords(mirror),
+        device_id_type=MESH,
+    )
+
+    for load in loads[:2]:
+        load.wait()
+    pl.semaphore_wait(barrier, half)
+    across.start()
+    pl.semaphore_signal(ready_sem, inc=1, device_id=coords(mirror), device_id_type=MESH)
+
+    def send_idx(k, c):
+        idx_copy(k).start()
+        return c
+
+    lax.fori_loop(1, half, send_idx, 0)
+    asked_vmem[me] = source_ref[...]
+
+    for load in loads[2:]:
         load.wait()
 
     def weigh(c, carry):
@@ -103,46 +173,6 @@
 
     lax.fori_loop(0, clusters, weigh, 0, unroll=8)
 
-    width = asked_vmem.shape[2]
-
-    def lane_base(p):
-        if links == width:
-            return 0
-        return pl.multiple_of(p * slots // width * width, width)
-
-    def idx_copy(k):
-        p = (me + k) % n
-        return pltpu.make_async_remote_copy(
-            src_ref=source_ref.at[:, pl.ds(lane_base(p), width)],
-            dst_ref=asked_vmem.at[me],
-            send_sem=send_sems.at[0],
-            recv_sem=idx_sem.at[k],
-            device_id=coords(p),
-            device_id_type=MESH,
-        )
-
-    def bwd_copy(k):
-        p = (me + k) % n
-        return pltpu.make_async_remote_copy(
-            src_ref=bwd_ref.at[pl.ds(p * slots, slots)],
-            dst_ref=arrived_hbm.at[pl.ds(me * slots, slots)],
-            send_sem=send_sems.at[1],
-            recv_sem=bwd_sem.at[k],
-            device_id=coords(p),
-            device_id_type=MESH,
-        )
-
-    def rad_copy(k):
-        p = (me + k) % n
-        return pltpu.make_async_remote_copy(
-            src_ref=served_ref.at[pl.ds(p * slots, slots)],
-            dst_ref=fetched_ref.at[pl.ds(me * slots, slots)],
-            send_sem=send_sems.at[2],
-            recv_sem=rad_sem.at[k],
-            device_id=coords(p),
-            device_id_type=MESH,
-        )
-
     def live_of(p, s):
         return jnp.where(s < count_ref[0, p], 1.0, 0.0).astype(F32)
 
@@ -151,7 +181,7 @@
 
     def back(t):
         for u in range(GROUP):
-            p = (me + 1 + t * GROUP + u) % n
+            p = peer(t * GROUP + u)
             for s in range(slots):
                 l = p * slots + s
                 form = form_ref[block_ref[0, l]]
@@ -159,83 +189,70 @@
                 got = jnp.dot(seen, form, preferred_element_type=F32)
                 bwd_ref[l] = (got * live_of(p, s)).astype(BF16)
 
-    def back_only(t, c):
-        back(t)
-        return c
-
-    def send_bwd(k, c):
-        bwd_copy(k).start()
-        return c
-
     def back_send(t, c):
         back(t)
         for u in range(GROUP):
-            k = 1 + t * GROUP + u
-
-            @pl.when(k != n)
+            k = t * GROUP + u
+
+            @pl.when(k != 0)
             def _():
                 bwd_copy(k).start()
 
         return c
 
-    early = n // GROUP // 2
-    lax.fori_loop(0, early, back_only, 0)
-    pl.semaphore_wait(barrier, n - 1)
-
-    def send_idx(k, c):
-        idx_copy(k).start()
-        return c
-
-    lax.fori_loop(1, n, send_idx, 0)
-    lax.fori_loop(1, 1 + early * GROUP, send_bwd, 0)
-    asked_vmem[me] = source_ref[:, pl.ds(lane_base(me), width)]
-    lax.fori_loop(early, n // GROUP, back_send, 0)
-
+    def serve(k, c, table_ref, owner):
+        p = near + (mine + k) % half
+        for s in range(slots):
+            served_ref[k * slots + s] = table_ref[asked_ref[p, 0, owner * slots + s]]
+
+        @pl.when(k % half != 0)
+        def _():
+            rad_copy(k).start()
+
+        return c
+
+    groups = half // GROUP
+    lax.fori_loop(0, groups, back_send, 0)
     own = pl.ds(me * slots, slots)
     keep_own = pltpu.make_async_copy(bwd_ref.at[own], arrived_hbm.at[own], out_sem.at[0])
     keep_own.start()
 
+    pl.semaphore_wait(ready_sem, 1)
+    lax.fori_loop(half, n, send_idx, 0)
+    lax.fori_loop(groups, 2 * groups, back_send, 0)
+
     def wait_idx(k, c):
         idx_copy(k).wait_recv()
         return c
 
-    lax.fori_loop(1, n, wait_idx, 0)
-    to_smem = pltpu.make_async_copy(asked_vmem, asked_ref, out_sem.at[1])
+    lax.fori_loop(1, half, wait_idx, 0)
+    side = pl.ds(near, half)
+    to_smem = pltpu.make_async_copy(asked_vmem.at[side], asked_ref.at[side], out_sem.at[1])
     to_smem.start()
     to_smem.wait()
-    base = me * slots % width
-
-    def serve(k, c):
-        p = (me + k) % n
-        for s in range(slots):
-            served_ref[p * slots + s] = rad_ref[asked_ref[p, 0, base + s]]
-
-        @pl.when(k != n)
-        def _():
-            rad_copy(k).start()
-
-        return c
-
-    lax.fori_loop(1, n + 1, serve, 0)
+    lax.fori_loop(0, half, functools.partial(serve, table_ref=rad_ref, owner=me), 0)
     for s in range(slots):
-        fetched_ref[me * slots + s] = served_ref[me * slots + s]
-    keep_asked = pltpu.make_async_copy(asked_vmem, asked_hbm, out_sem.at[1])
-    keep_asked.start()
-
-    def fwd_copy(k):
-        mine = pl.ds((me + n - k) % n * slots, slots)
-        return pltpu.make_async_copy(fwd_ref.at[mine], fwd_hbm.at[mine], out_sem.at[2])
-
-    def forward(t, c):
+        fetched_ref[me * slots + s] = served_ref[s]
+
+    def fwd_copy(k, host):
+        p = near + (mine + half - k) % half
+        rows = pl.ds(jnp.where(host, p, mirror_of(p)) * slots, slots)
+        return pltpu.make_async_copy(fwd_ref.at[rows], fwd_hbm.at[rows], out_sem.at[2])
+
+    def forward(t, c, host):
+        base = 0 if host else half
         for u in range(GROUP):
             k = t * GROUP + u
 
             @pl.when(k != 0)
             def _():
-                rad_copy(k).wait_recv()
+                rad_copy(base + k).wait_recv()
 
         for u in range(GROUP):
-            p = (me + n - t * GROUP - u) % n
+            k = t * GROUP + u
+            p = near + (mine + half - k) % half
+            if not host:
+                p = mirror_of(p)
             for s in range(slots):
                 l = p * slots + s
                 form = form_ref[block_ref[0, l]]
@@ -244,10 +261,20 @@
                 )
                 fwd_ref[l] = got * live_of(p, s)
         for u in range(GROUP):
-            fwd_copy(t * GROUP + u).start()
-        return c
-
-    lax.fori_loop(0, n // GROUP, forward, 0)
+            fwd_copy(t * GROUP + u, host).start()
+        return c
+
+    across.wait_recv()
+    lax.fori_loop(half, n, functools.partial(serve, table_ref=mirrored_ref, owner=mirror), 0)
+    for s in range(slots):
+        fetched_ref[mirror * slots + s] = served_ref[half * slots + s]
+
+    lax.fori_loop(0, groups, functools.partial(forward, host=True), 0)
+    lax.fori_loop(0, groups, functools.partial(forward, host=False), 0)
+
+    lax.fori_loop(half, n, wait_idx, 0)
+    keep_asked = pltpu.make_async_copy(asked_vmem, asked_hbm, out_sem.at[1])
+    keep_asked.start()
 
     def wait_bwd(k, c):
         bwd_copy(k).wait_recv()
@@ -255,10 +282,12 @@
 
     lax.fori_loop(1, n, wait_bwd, 0)
     most = pl.ds(0, (n - 1) * slots)
-    for buf, which in ((bwd_ref, 1), (served_ref, 2)):
-        pltpu.make_async_copy(buf.at[most], buf.at[most], send_sems.at[which]).wait()
+    pltpu.make_async_copy(bwd_ref.at[most], bwd_ref.at[most], send_sems.at[1]).wait()
+    most = pl.ds(0, (n - 2) * slots)
+    pltpu.make_async_copy(served_ref.at[most], served_ref.at[most], send_sems.at[2]).wait()
     rows = asked_vmem.at[pl.ds(0, n - 1)]
     pltpu.make_async_copy(rows, rows, send_sems.at[0]).wait()
+    across.wait_send()
     keep_own.wait()
     keep_asked.wait()
     pltpu.make_async_copy(fwd_ref, fwd_hbm, out_sem.at[2]).wait()
@@ -292,8 +321,7 @@
     clusters = em_ref.shape[0]
     links = fwd_ref.shape[0]
     slots = links // n
-    width = asked_ref.shape[2]
-    base = me * slots % width
+    base = me * slots
     parts = out_sem.shape[0]
     step = clusters // parts
     loads = [
@@ -370,14 +398,13 @@
         slots = links // n
         tile = (bands, patches)
         hbm = pl.BlockSpec(memory_space=pl.ANY)
-        width = min(links, LANES)
         parts = 4
         fwd, arrived, asked = pl.pallas_call(
-            functools.partial(exchange, n, inner),
+            functools.partial(exchange, outer, inner),
             out_shape=(
                 jax.ShapeDtypeStruct((links,) + tile, F32),
                 jax.ShapeDtypeStruct((links,) + tile, BF16),
-                jax.ShapeDtypeStruct((n, 1, width), jnp.int32),
+                jax.ShapeDtypeStruct((n, 1, links), jnp.int32),
             ),
             in_specs=[hbm] * 7,
             out_specs=(hbm, hbm, hbm),
@@ -390,16 +417,19 @@
                 pltpu.VMEM(patch_area.shape, F32),
                 pltpu.VMEM(form_factor.shape, BF16),
                 pltpu.VMEM((clusters,) + tile, BF16),
+                pltpu.VMEM((clusters,) + tile, BF16),
                 pltpu.VMEM((links,) + tile, BF16),
                 pltpu.VMEM((links,) + tile, BF16),
                 pltpu.VMEM((links,) + tile, BF16),
                 pltpu.VMEM((links,) + tile, F32),
-                pltpu.VMEM((n, 1, width), jnp.int32),
-                pltpu.SMEM((n, 1, width), jnp.int32),
+                pltpu.VMEM((n, 1, links), jnp.int32),
+                pltpu.SMEM((n, 1, links), jnp.int32),
                 pltpu.SemaphoreType.DMA((parts,)),
                 pltpu.SemaphoreType.DMA((6,)),
                 pltpu.SemaphoreType.DMA((3,)),
                 pltpu.SemaphoreType.DMA((3,)),
+                pltpu.SemaphoreType.REGULAR,
+                pltpu.SemaphoreType.DMA((2,)),
                 pltpu.SemaphoreType.DMA((n,)),
                 pltpu.SemaphoreType.DMA((n,)),
                 pltpu.SemaphoreType.DMA((n,)),
@@ -427,7 +457,7 @@
                 pltpu.VMEM((clusters,) + tile, F32),
                 pltpu.VMEM(patch_area.shape, F32),
                 pltpu.SMEM(target_index.shape, jnp.int32),
-                pltpu.SMEM((n, 1, width), jnp.int32),
+                pltpu.SMEM((n, 1, links), jnp.int32),
                 pltpu.VMEM((links,) + tile, F32),
                 pltpu.VMEM((links,) + tile, BF16),
                 pltpu.VMEM((clusters,) + tile, F32),

time: 35.9 us -> 35.5 us (0.989)
  Pallas kernels: 35.5 us -> 35 us
    pallas_call x1, Pallas kernels: 32.5 us -> 32 us  [shards(): pl.pallas_call(functools.partial(exchange, outer, inner), out_shape=(jax....]
where the time goes in v1:
time: 35.5 us; the launch traced here: 35 us
  Pallas kernels  35 us (99%)
    pallas_call x1, Pallas kernels, shards(): pl.pallas_call(functools.partial(exchange, outer, inner), out_shape=(jax....  32 us
    pallas_call x1, Pallas kernels, shards(): pl.pallas_call(functools.partial(combine, n, inner), out_shape=jax.ShapeD...  2.93 us

profile of v1, /device:TPU:1, one launch (start us, length us, event | category | flops | bytes accessed | tf_op | source)
XLA Modules:
  0.0 35.0 jit_solution(15426629495044474997)
XLA Ops:
  0.0 32.0 %exchange.1 = (f32[128,16,128]{2,1,0:T(8,128)}, bf16[128,16,128]{2,1,0:T(8,128)(2,1)}, s32[32,1,128]{2,1,0:T(1,128)}) custom-call(s32[1,128]{1,0:T(1,128)} %block_hbm.1, s32[1,128]{1,0:T(1,128)} %target_hbm.3, s32[1,32]{1,0:T(1,128)} %count_hbm.1, s32[1,128]{1,0:T(1,128)} %source_hbm.1, bf16[64,16,128]{2,1,0:T(8,128)(2,1)} %rad_hbm.1, f32[64,128]{1,0:T(8,128)} %area_hbm.3, ...), custom_call_target="tpu_custom_call" | custom-call | tf_op jit(solution)/shard_map/exchange/pallas_call | solution.py:402
  32.0 2.9 %combine.1 = f32[64,16,128]{2,1,0:T(8,128)} custom-call(s32[1,128]{1,0:T(1,128)} %target_hbm.3, s32[32,1,128]{2,1,0:T(1,128)} %get-tuple-element.8.asked_hbm, f32[128,16,128]{2,1,0:T(8,128)} %get-tuple-element.9.fwd_hbm, bf16[128,16,128]{2,1,0:T(8,128)(2,1)} %get-tuple-element.10.arrived_hbm, f32[64,16,128]{2,1,0:T(8,128)} %em_hbm.1, ...), custom_call_target="tpu_custom_call" | custom-call | tf_op jit(solution)/shard_map/combine/pallas_call | solution.py:450

commit v2 on v1

v2 whole, which is shorter than its diff:
```python
import functools

import jax
import jax.numpy as jnp
from jax import lax
from jax.experimental import pallas as pl
from jax.experimental.pallas import tpu as pltpu
from jax.sharding import PartitionSpec as P

MESH = pl.DeviceIdType.MESH
GROUP = 4
EXCHANGE_MIB = 60
F32 = jnp.float32
BF16 = jnp.bfloat16


def exchange(
    outer,
    inner,
    block_hbm,
    target_hbm,
    count_hbm,
    source_hbm,
    rad_hbm,
    area_hbm,
    form_hbm,
    em_hbm,
    refl_hbm,
    out_ref,
    block_ref,
    target_ref,
    count_ref,
    source_ref,
    rad_ref,
    area_ref,
    form_ref,
    mirrored_ref,
    weighted_ref,
    bwd_ref,
    served_ref,
    fetched_ref,
    arrived_ref,
    gath_ref,
    ret_ref,
    em_ref,
    refl_ref,
    asked_vmem,
    asked_ref,
    keys_ref,
    chain_vmem,
    chain_ref,
    form_sem,
    in_sem,
    out_sem,
    send_sems,
    ready_sem,
    mirror_sem,
    idx_sem,
    bwd_sem,
    rad_sem,
):
    n = outer * inner
    half = n // 2
    gx, gy = lax.axis_index("gx"), lax.axis_index("gy")
    me = gx * inner + gy
    mine = me % half
    near = me // half * half
    far = half - near
    mirror = (outer - 1 - gx) * inner + gy
    links = block_ref.shape[1]
    slots = links // n
    clusters = rad_ref.shape[0]
    lanes = keys_ref.shape[1]
    parts = form_sem.shape[0]
    step = links // parts

    def coords(p):
        return (p // inner, p % inner)

    def mirror_of(p):
        return (outer - 1 - p // inner) * inner + p % inner

    def peer(k):
        return near + (mine + k) % half

    def far_peer(k):
        plane = k // inner
        return jnp.where(near == 0, outer - 1 - plane, plane) * inner + (gy + k) % inner

    loads = [
        pltpu.make_async_copy(src, dst, in_sem.at[i])
        for i, (src, dst) in enumerate(
            (
                (rad_hbm, rad_ref),
                (source_hbm, source_ref),
                (area_hbm, area_ref),
                (block_hbm, block_ref),
                (target_hbm, target_ref),
                (count_hbm, count_ref),
                (em_hbm, em_ref),
                (refl_hbm, refl_ref),
            )
        )
    ]
    forms = [
        pltpu.make_async_copy(
            form_hbm.at[pl.ds(i * step, step)], form_ref.at[pl.ds(i * step, step)], form_sem.at[i]
        )
        for i in range(parts)
    ]
    for load in loads[:6] + forms + loads[6:]:
        load.start()

    barrier = pltpu.get_barrier_semaphore()
    pl.semaphore_signal(barrier, inc=1, device_id=coords(mirror), device_id_type=MESH)

    def greet(k, c):
        pl.semaphore_signal(barrier, inc=1, device_id=coords(peer(k)), device_id_type=MESH)
        return c

    lax.fori_loop(1, half, greet, 0)

    def idx_copy(to, sender=me, src_ref=source_ref):
        return pltpu.make_async_remote_copy(
            src_ref=src_ref,
            dst_ref=asked_vmem.at[sender],
            send_sem=send_sems.at[0],
            recv_sem=idx_sem.at[sender],
            device_id=coords(to),
            device_id_type=MESH,
        )

    def bwd_copy(to, sender=me):
        return pltpu.make_async_remote_copy(
            src_ref=bwd_ref.at[pl.ds(to * slots, slots)],
            dst_ref=arrived_ref.at[pl.ds(sender * slots, slots)],
            send_sem=send_sems.at[1],
            recv_sem=bwd_sem.at[sender],
            device_id=coords(to),
            device_id_type=MESH,
        )

    def rad_copy(to, owner, row):
        return pltpu.make_async_remote_copy(
            src_ref=served_ref.at[pl.ds(row * slots, slots)],
            dst_ref=fetched_ref.at[pl.ds(owner * slots, slots)],
            send_sem=send_sems.at[2],
            recv_sem=rad_sem.at[owner],
            device_id=coords(to),
            device_id_type=MESH,
        )

    share = clusters // mirror_sem.shape[1]
    across = [
        pltpu.make_async_remote_copy(
            src_ref=rad_ref.at[pl.ds(i * share, share)],
            dst_ref=mirrored_ref.at[pl.ds(i * share, share)],
            send_sem=mirror_sem.at[0, i],
            recv_sem=mirror_sem.at[1, i],
            device_id=coords(mirror),
            device_id_type=MESH,
        )
        for i in range(mirror_sem.shape[1])
    ]

    def send_idx(k, c):
        idx_copy(peer(k)).start()
        return c

    def relay_idx(k, c):
        idx_copy(peer(k), mirror, asked_vmem.at[mirror]).start()
        return c

    for load in loads[:2]:
        load.wait()
    pl.semaphore_wait(barrier, half)
    idx_copy(mirror).start()
    lax.fori_loop(1, half, send_idx, 0)
    for copy in across:
        copy.start()
    pl.semaphore_signal(ready_sem, inc=1, device_id=coords(mirror), device_id_type=MESH)
    asked_vmem[me] = source_ref[...]

    for load in loads[2:6]:
        load.wait()

    def weigh(c, carry):
        area = area_ref[pl.ds(c, 1), :]
        weighted_ref[c] = (area * rad_ref[c].astype(F32)).astype(BF16)
        return carry

    lax.fori_loop(0, clusters, weigh, 0, unroll=8)

    def live_of(p, s):
        return jnp.where(s < count_ref[0, p], 1.0, 0.0).astype(F32)

    for form in forms:
        form.wait()

    def back(p):
        for s in range(slots):
            l = p * slots + s
            form = form_ref[block_ref[0, l]]
            seen = weighted_ref[target_ref[0, l]]
            got = jnp.dot(seen, form, preferred_element_type=F32)
            bwd_ref[l] = (got * live_of(p, s)).astype(BF16)

    def back_near(t, c):
        for u in range(GROUP):
            back(peer(t * GROUP + u))
        for u in range(GROUP):
            k = t * GROUP + u

            @pl.when(k != 0)
            def _():
                bwd_copy(peer(k)).start()

        return c

    def back_far(t, c):
        for u in range(GROUP):
            back(far_peer(t * GROUP + u))
        return c

    def send_far(k, c):
        bwd_copy(far_peer(k)).start()
        return c

    def serve(k, c, table_ref, owner, base):
        p = peer(k)
        for s in range(slots):
            served_ref[(base + k) * slots + s] = table_ref[asked_ref[p, 0, owner * slots + s]]

        @pl.when(k != 0)
        def _():
            rad_copy(p, owner, base + k).start()

        return c

    groups = half // GROUP
    lax.fori_loop(0, groups, back_near, 0)
    for s in range(slots):
        arrived_ref[me * slots + s] = bwd_ref[me * slots + s]
    lax.fori_loop(0, groups, back_far, 0)

    def wait_idx(k, c):
        idx_copy(me, peer(k)).wait_recv()
        return c

    def wait_idx_far(k, c):
        idx_copy(me, mirror_of(peer(k))).wait_recv()
        return c

    idx_copy(me, mirror).wait_recv()
    lax.fori_loop(1, half, relay_idx, 0)
    lax.fori_loop(1, half, wait_idx, 0)
    side = pl.ds(near, half)
    to_smem = pltpu.make_async_copy(asked_vmem.at[side], asked_ref.at[side], out_sem.at[2])
    to_smem.start()
    to_smem.wait()
    lax.fori_loop(0, half, functools.partial(serve, table_ref=rad_ref, owner=me, base=0), 0)
    for s in range(slots):
        fetched_ref[me * slots + s] = served_ref[s]

    pl.semaphore_wait(ready_sem, 1)
    for copy in across[:-1]:
        copy.wait_send()
    lax.fori_loop(0, half, send_far, 0)

    def link_chain(near_key, far_key, row):
        def fill(k, c, key, base):
            for s in range(slots):
                keys_ref[pl.ds((base + k) * slots + s, 1), :] = jnp.full((1, lanes), key(k, s), jnp.int32)
            return c

        lax.fori_loop(0, half, functools.partial(fill, key=near_key, base=0), 0, unroll=2)
        lax.fori_loop(0, half, functools.partial(fill, key=far_key, base=half), 0, unroll=2)
        keys = keys_ref[...]
        order = lax.broadcasted_iota(jnp.int32, keys.shape, 0)
        lane = lax.broadcasted_iota(jnp.int32, keys.shape, 1)
        for i in range(links // lanes):
            at = lane + i * lanes
            key = jnp.max(jnp.where(order == at, keys, -1), axis=0, keepdims=True)
            before = jnp.max(
                jnp.where((keys == key) & (order < at), order, -1), axis=0, keepdims=True
            )
            chain_vmem[row, :, pl.ds(i * lanes, lanes)] = jnp.where(before < 0, links, before)
        last = jnp.max(jnp.where(keys == lane, order, -1), axis=0, keepdims=True)
        chain_vmem[row + 1, :, pl.ds(0, lanes)] = jnp.where(last < 0, links, last)
        rows = pl.ds(row, 2)
        return pltpu.make_async_copy(chain_vmem.at[rows], chain_ref.at[rows], out_sem.at[row // 2])

    def summed(ref, row, at):
        return ref[chain_ref[row, 0, at]]

    def target_key(k, s):
        return target_ref[0, peer(k) * slots + s]

    def target_key_far(k, s):
        return target_ref[0, mirror_of(peer(k)) * slots + s]

    def source_key(k, s):
        return asked_ref[peer(k), 0, me * slots + s]

    def source_key_far(k, s):
        return asked_ref[far_peer(k), 0, me * slots + s]

    def forward(t, c, host):
        owners = [peer(t * GROUP + u) for u in range(GROUP)]
        if not host:
            owners = [mirror_of(p) for p in owners]
        for u, p in enumerate(owners):

            @pl.when(t * GROUP + u != 0)
            def _():
                rad_copy(me, p, 0).wait_recv()

        got = []
        for p in owners:
            for s in range(slots):
                l = p * slots + s
                form = form_ref[block_ref[0, l]]
                seen = lax.dot_general(
                    fetched_ref[l], form, (((1,), (1,)), ((), ())), preferred_element_type=F32
                )
                got.append(seen * live_of(p, s))
        first = ((0 if host else half) + t * GROUP) * slots
        for i, term in enumerate(got):
            gath_ref[first + i] = term + summed(gath_ref, 0, first + i)
        return c

    gath_ref[links] = jnp.zeros(gath_ref.shape[1:], F32)
    ret_ref[links] = jnp.zeros(ret_ref.shape[1:], F32)
    by_target = link_chain(target_key, target_key_far, 0)
    by_target.start()
    lax.fori_loop(1, half, wait_idx_far, 0)
    beyond = pl.ds(far, half)
    to_smem = pltpu.make_async_copy(asked_vmem.at[beyond], asked_ref.at[beyond], out_sem.at[2])
    to_smem.start()
    to_smem.wait()
    by_source = link_chain(source_key, source_key_far, 2)
    by_source.start()
    by_target.wait()

    by_source.wait()

    for copy in across:
        copy.wait_recv()
    lax.fori_loop(
        0, half, functools.partial(serve, table_ref=mirrored_ref, owner=mirror, base=half), 0
    )
    for s in range(slots):
        fetched_ref[mirror * slots + s] = served_ref[half * slots + s]

    lax.fori_loop(0, groups, functools.partial(forward, host=True), 0)
    lax.fori_loop(0, groups, functools.partial(forward, host=False), 0)

    def blend(c, carry):
        area = area_ref[pl.ds(c, 1), :]
        em_ref[c] = em_ref[c] + refl_ref[c] * summed(gath_ref, 1, c)
        refl_ref[c] = refl_ref[c] / area
        return carry

    for load in loads[6:]:
        load.wait()
    lax.fori_loop(0, clusters, blend, 0, unroll=8)

    def collect(k, c, peers, base, skip):
        p = peers(k)

        @pl.when(k != skip)
        def _():
            bwd_copy(me, p).wait_recv()

        for s in range(slots):
            i = (base + k) * slots + s
            ret_ref[i] = arrived_ref[p * slots + s].astype(F32) + summed(ret_ref, 2, i)
        return c

    lax.fori_loop(0, half, functools.partial(collect, peers=peer, base=0, skip=0), 0)
    lax.fori_loop(0, half, functools.partial(collect, peers=far_peer, base=half, skip=half), 0)

    def finish(c, carry):
        out_ref[c] = em_ref[c] + refl_ref[c] * summed(ret_ref, 3, c)
        return carry

    lax.fori_loop(0, clusters, finish, 0, unroll=8)
    most = pl.ds(0, (n - 1) * slots)
    pltpu.make_async_copy(bwd_ref.at[most], bwd_ref.at[most], send_sems.at[1]).wait()
    most = pl.ds(0, (n - 2) * slots)
    pltpu.make_async_copy(served_ref.at[most], served_ref.at[most], send_sems.at[2]).wait()
    rows = asked_vmem.at[pl.ds(0, n - 1)]
    pltpu.make_async_copy(rows, rows, send_sems.at[0]).wait()
    across[-1].wait_send()


def solution(mesh):
    outer, inner = mesh.shape["gx"], mesh.shape["gy"]
    n = outer * inner

    def shards(
        radiance,
        emission,
        reflectance,
        patch_area,
        form_factor,
        source_index,
        target_index,
        block_index,
        valid_count,
    ):
        clusters, bands, patches = radiance.shape
        links = source_index.shape[1]
        slots = links // n
        tile = (bands, patches)
        hbm = pl.BlockSpec(memory_space=pl.ANY)
        parts = 4
        return pl.pallas_call(
            functools.partial(exchange, outer, inner),
            out_shape=pltpu.VMEM((clusters,) + tile, F32),
            in_specs=[hbm] * 9,
            out_specs=pl.BlockSpec(memory_space=pltpu.VMEM),
            scratch_shapes=[
                pltpu.SMEM(block_index.shape, jnp.int32),
                pltpu.SMEM(target_index.shape, jnp.int32),
                pltpu.SMEM(valid_count.shape, jnp.int32),
                pltpu.VMEM(source_index.shape, jnp.int32),
                pltpu.VMEM(radiance.shape, BF16),
                pltpu.VMEM(patch_area.shape, F32),
                pltpu.VMEM(form_factor.shape, BF16),
                pltpu.VMEM((clusters,) + tile, BF16),
                pltpu.VMEM((clusters,) + tile, BF16),
                pltpu.VMEM((links,) + tile, BF16),
                pltpu.VMEM((links,) + tile, BF16),
                pltpu.VMEM((links,) + tile, BF16),
                pltpu.VMEM((links,) + tile, BF16),
                pltpu.VMEM((links + 1,) + tile, F32),
                pltpu.VMEM((links + 1,) + tile, F32),
                pltpu.VMEM((clusters,) + tile, F32),
                pltpu.VMEM((clusters,) + tile, F32),
                pltpu.VMEM((n, 1, links), jnp.int32),
                pltpu.SMEM((n, 1, links), jnp.int32),
                pltpu.VMEM((links, patches), jnp.int32),
                pltpu.VMEM((4, 1, links), jnp.int32),
                pltpu.SMEM((4, 1, links), jnp.int32),
                pltpu.SemaphoreType.DMA((parts,)),
                pltpu.SemaphoreType.DMA((8,)),
                pltpu.SemaphoreType.DMA((3,)),
                pltpu.SemaphoreType.DMA((3,)),
                pltpu.SemaphoreType.REGULAR,
                pltpu.SemaphoreType.DMA((2, 4)),
                pltpu.SemaphoreType.DMA((n,)),
                pltpu.SemaphoreType.DMA((n,)),
                pltpu.SemaphoreType.DMA((n,)),
            ],
            compiler_params=pltpu.CompilerParams(
                collective_id=0, has_side_effects=True, vmem_limit_bytes=EXCHANGE_MIB * 1024 * 1024
            ),
            name="exchange",
        )(
            block_index,
            target_index,
            valid_count,
            source_index,
            radiance,
            patch_area,
            form_factor,
            emission,
            reflectance,
        )

    spec3 = P(("gx", "gy"), None, None)
    spec2 = P(("gx", "gy"), None)
    return jax.shard_map(
        shards,
        mesh=mesh,
        in_specs=(spec3, spec3, spec3, spec2, spec3, spec2, spec2, spec2, spec2),
        out_specs=spec3,
        check_vma=False,
    )
```

time: 35.5 us -> 31.2 us (0.88)
  the two profiles are of different devices: /device:TPU:1 before, /device:TPU:11 now
where the time goes in v2:
time: 31.2 us; the launch traced here: 31.1 us
  Pallas kernels  30.2 us (97%)
  local copies, waits for them, and re-layouts  0.8 us (3%)
    pallas_call x1, Pallas kernels, shards(): pl.pallas_call(functools.partial(exchange, outer, inner), out_shape=pltpu...  30.2 us
    unnamed x1, local copies, waits for them, and re-layouts  0.8 us

profile of v2, /device:TPU:11, one launch (start us, length us, event | category | flops | bytes accessed | tf_op | source)
XLA Modules:
  0.0 31.1 jit_solution(11713016342786432719)
XLA Ops:
  0.0 30.2 %exchange.1 = f32[64,16,128]{2,1,0:T(8,128)S(1)} custom-call(s32[1,128]{1,0:T(1,128)} %block_hbm.1, s32[1,128]{1,0:T(1,128)} %target_hbm.1, s32[1,32]{1,0:T(1,128)} %count_hbm.1, s32[1,128]{1,0:T(1,128)} %source_hbm.1, bf16[64,16,128]{2,1,0:T(8,128)(2,1)} %rad_hbm.1, f32[64,128]{1,0:T(8,128)} %area_hbm.1, bf16[128,128,128]{2,1,0:T(8,128)(2,1)} %form_hbm.1, ...), custom_call_target="tpu_custom_call" | custom-call | tf_op jit(solution)/shard_map/exchange/pallas_call | solution.py:418
  30.3 0.8 %copy.11 = f32[64,16,128]{2,1,0:T(8,128)} copy(f32[64,16,128]{2,1,0:T(8,128)S(1)} %exchange.1) | data formatting | bytes 1048576

commit v3 on v2

v3 whole, which is shorter than its diff:
```python
import functools

import jax
import jax.numpy as jnp
from jax import lax
from jax.experimental import pallas as pl
from jax.experimental.pallas import tpu as pltpu
from jax.sharding import PartitionSpec as P

MESH = pl.DeviceIdType.MESH
GROUP = 4
EXCHANGE_MIB = 60
F32 = jnp.float32
BF16 = jnp.bfloat16


def exchange(
    outer,
    inner,
    block_hbm,
    target_hbm,
    count_hbm,
    source_hbm,
    rad_hbm,
    area_hbm,
    form_hbm,
    em_hbm,
    refl_hbm,
    out_ref,
    block_ref,
    target_ref,
    count_ref,
    source_ref,
    rad_ref,
    area_ref,
    form_ref,
    tables,
    weighted_ref,
    bwd_ref,
    served_ref,
    fetched_ref,
    arrived_ref,
    gath_ref,
    ret_ref,
    em_ref,
    refl_ref,
    part_ref,
    asked_vmem,
    asked_ref,
    keys_ref,
    chain_vmem,
    chain_ref,
    form_sem,
    in_sem,
    out_sem,
    send_sems,
    ready_sem,
    round_sem,
    mirror_sem,
    idx_sem,
    bwd_sem,
    rad_sem,
):
    n = outer * inner
    half = n // 2
    gx, gy = lax.axis_index("gx"), lax.axis_index("gy")
    me = gx * inner + gy
    mine = me % half
    near = me // half * half
    far = half - near
    planes = outer // 2
    depth = jnp.where(near == 0, gx, outer - 1 - gx)
    is_gate = depth == planes - 1
    gate = jnp.where(near == 0, planes, planes - 1) * inner + gy
    links = block_ref.shape[1]
    slots = links // n
    clusters = rad_ref.shape[0]
    lanes = keys_ref.shape[1]
    parts = 4
    step = links // parts
    groups = half // GROUP

    def coords(p):
        return (p // inner, p % inner)

    def peer(k):
        return near + (mine + k) % half

    def far_plane(j):
        return jnp.where(near == 0, outer - 1 - j, j) * inner

    def far_peer(k):
        return far_plane(k // inner) + (gy + k) % inner

    loads = [
        pltpu.make_async_copy(src, dst, in_sem.at[i])
        for i, (src, dst) in enumerate(
            (
                (rad_hbm, rad_ref),
                (source_hbm, source_ref),
                (area_hbm, area_ref),
                (block_hbm, block_ref),
                (target_hbm, target_ref),
                (count_hbm, count_ref),
                (em_hbm, em_ref),
                (refl_hbm, refl_ref),
            )
        )
    ]
    forms = [
        pltpu.make_async_copy(
            form_hbm.at[pl.ds(i * step, step)], form_ref.at[pl.ds(i * step, step)], form_sem
        )
        for i in range(parts)
    ]
    for load in loads[:6] + forms + loads[6:]:
        load.start()

    def beside(j):
        bit = 1 << j
        return near + mine + bit - 2 * bit * (mine // bit % 2)

    barrier = pltpu.get_barrier_semaphore()
    bits = half.bit_length() - 1
    for j in range(bits):
        pl.semaphore_signal(barrier, inc=1, device_id=coords(beside(j)), device_id_type=MESH)

    @pl.when(is_gate)
    def _():
        for j in range(planes):
            pl.semaphore_signal(
                barrier, inc=1, device_id=coords(far_plane(j) + gy), device_id_type=MESH
            )

    def settle(ref, rows, sem):
        part = ref.at[pl.ds(0, rows)]
        pltpu.make_async_copy(part, part, sem).wait()

    def idx_copy(to, which, sender=me, src_ref=source_ref):
        return pltpu.make_async_remote_copy(
            src_ref=src_ref,
            dst_ref=asked_vmem.at[sender],
            send_sem=send_sems.at[0],
            recv_sem=idx_sem.at[which],
            device_id=coords(to),
            device_id_type=MESH,
        )

    def bwd_copy(to, which):
        return pltpu.make_async_remote_copy(
            src_ref=bwd_ref.at[pl.ds(to * slots, slots)],
            dst_ref=arrived_ref.at[pl.ds(me * slots, slots)],
            send_sem=send_sems.at[1],
            recv_sem=bwd_sem.at[which],
            device_id=coords(to),
            device_id_type=MESH,
        )

    def rad_copy(to, owner, row, which):
        return pltpu.make_async_remote_copy(
            src_ref=served_ref.at[pl.ds(row * slots, slots)],
            dst_ref=fetched_ref.at[pl.ds(owner * slots, slots)],
            send_sem=send_sems.at[2],
            recv_sem=rad_sem.at[which],
            device_id=coords(to),
            device_id_type=MESH,
        )

    pieces = 4
    share = clusters // pieces
    def across(i, j):
        part = pl.ds(i * share, share)
        return pltpu.make_async_remote_copy(
            src_ref=rad_ref.at[part],
            dst_ref=tables[j].at[part],
            send_sem=mirror_sem.at[0 if i < pieces - 1 else 1],
            recv_sem=mirror_sem.at[2 + j],
            device_id=coords(gate),
            device_id_type=MESH,
        )

    def send_pieces(first, end):
        for j in range(planes):

            @pl.when(depth == j)
            def _():
                for i in range(first, end):
                    across(i, j).start()

    def send_idx(k, c):
        idx_copy(peer(k), 0).start()
        return c

    def relay_idx(k, c):
        for j in range(planes):
            owner = far_plane(j) + gy
            idx_copy(peer(k), 2, owner, asked_vmem.at[owner]).start()
        return c

    def tell(j):
        pl.semaphore_signal(round_sem.at[j], inc=1, device_id=coords(beside(j)), device_id_type=MESH)

    for load in loads[:2]:
        load.wait()
    pl.semaphore_wait(barrier, bits + 1)
    idx_copy(gate, 1).start()
    send_pieces(0, pieces // 2)
    tell(0)
    asked_vmem[me] = source_ref[...]
    for load in loads[2:6]:
        load.wait()
    for j in range(bits - 1):
        pl.semaphore_wait(round_sem.at[j], 1)
        if j + 1 < bits - 1:
            tell(j + 1)
    lax.fori_loop(1, half, send_idx, 0)

    @pl.when(is_gate)
    def _():
        pl.semaphore_signal(ready_sem, inc=1, device_id=coords(gate), device_id_type=MESH)

    send_pieces(pieces // 2, pieces)

    def weigh(c, carry):
        area = area_ref[pl.ds(c, 1), :]
        weighted_ref[c] = (area * rad_ref[c].astype(F32)).astype(BF16)
        return carry

    lax.fori_loop(0, clusters, weigh, 0, unroll=8)

    def live_of(p, s):
        return jnp.where(s < count_ref[0, p], 1.0, 0.0).astype(F32)

    pltpu.make_async_copy(form_hbm, form_ref, form_sem).wait()

    def back(p):
        for s in range(slots):
            l = p * slots + s
            form = form_ref[block_ref[0, l]]
            seen = weighted_ref[target_ref[0, l]]
            got = jnp.dot(seen, form, preferred_element_type=F32)
            bwd_ref[l] = (got * live_of(p, s)).astype(BF16)

    def back_near(t, c):
        for u in range(GROUP):
            back(peer(t * GROUP + u))
        return c

    def back_far(t, c):
        for u in range(GROUP):
            back(far_peer(t * GROUP + u))
        return c

    def send_near(k, c):
        bwd_copy(peer(k), 0).start()
        return c

    def send_far(k, c):
        at = depth * inner + (inner - k % inner) % inner
        bwd_copy(far_peer(k), 1 + at // GROUP).start()
        return c

    def serve(k, c):
        p = peer(k)
        for s in range(slots):
            served_ref[k * slots + s] = rad_ref[asked_ref[p, 0, me * slots + s]]

        @pl.when(k != 0)
        def _():
            rad_copy(p, me, k, (half - k) % half // GROUP).start()

        return c

    def serve_table(k, c, j):
        p = peer(k)
        owner = far_plane(j) + gy
        base = (1 + j) * half + k
        for s in range(slots):
            served_ref[base * slots + s] = tables[j][asked_ref[p, 0, owner * slots + s]]

        @pl.when(k != 0)
        def _():
            at = j * inner + (inner - k % inner) % inner
            rad_copy(p, owner, base, groups + at // GROUP).start()

        return c

    def open_table(j):
        settle(rad_ref, clusters, mirror_sem.at[2 + j])
        lax.fori_loop(0, half, functools.partial(serve_table, j=j), 0)
        owner = far_plane(j) + gy
        for s in range(slots):
            fetched_ref[owner * slots + s] = served_ref[(1 + j) * half * slots + s]

    lax.fori_loop(0, groups, back_near, 0)
    lax.fori_loop(1, half, send_near, 0)
    for s in range(slots):
        arrived_ref[me * slots + s] = bwd_ref[me * slots + s]
    lax.fori_loop(0, groups, back_far, 0)

    @pl.when(is_gate)
    def _():
        settle(asked_vmem, planes, idx_sem.at[1])
        lax.fori_loop(1, half, relay_idx, 0)

    settle(asked_vmem, half - 1, idx_sem.at[0])
    side = pl.ds(near, half)
    to_smem = pltpu.make_async_copy(asked_vmem.at[side], asked_ref.at[side], out_sem.at[2])
    to_smem.start()
    to_smem.wait()
    lax.fori_loop(0, half, serve, 0)
    for s in range(slots):
        fetched_ref[me * slots + s] = served_ref[s]

    @pl.when(is_gate)
    def _():
        for j in range(planes - 1):
            open_table(j)

    settle(rad_ref, clusters - share, mirror_sem.at[0])
    pl.semaphore_wait(ready_sem, 1)

    @pl.when(is_gate)
    def _():
        for j in range(1, planes):
            p = near + (mine + j * inner) % half
            pl.semaphore_signal(ready_sem, inc=1, device_id=coords(p), device_id_type=MESH)

    lax.fori_loop(0, half, send_far, 0)

    def link_chain(near_key, far_key, row):
        def fill(k, c, key, base):
            for s in range(slots):
                keys_ref[pl.ds((base + k) * slots + s, 1), :] = jnp.full((1, lanes), key(k, s), jnp.int32)
            return c

        lax.fori_loop(0, half, functools.partial(fill, key=near_key, base=0), 0, unroll=2)
        lax.fori_loop(0, half, functools.partial(fill, key=far_key, base=half), 0, unroll=2)
        keys = keys_ref[...]
        order = lax.broadcasted_iota(jnp.int32, keys.shape, 0)
        lane = lax.broadcasted_iota(jnp.int32, keys.shape, 1)
        for i in range(links // lanes):
            at = lane + i * lanes
            key = jnp.max(jnp.where(order == at, keys, -1), axis=0, keepdims=True)
            before = jnp.max(
                jnp.where((keys == key) & (order < at), order, -1), axis=0, keepdims=True
            )
            chain_vmem[row, :, pl.ds(i * lanes, lanes)] = jnp.where(before < 0, links, before)
        last = jnp.max(jnp.where(keys == lane, order, -1), axis=0, keepdims=True)
        chain_vmem[row + 1, :, pl.ds(0, lanes)] = jnp.where(last < 0, links, last)
        rows = pl.ds(row, 2)
        return pltpu.make_async_copy(chain_vmem.at[rows], chain_ref.at[rows], out_sem.at[row // 2])

    def summed(ref, row, at):
        return ref[chain_ref[row, 0, at]]

    def target_key(k, s):
        return target_ref[0, peer(k) * slots + s]

    def target_key_far(k, s):
        return target_ref[0, far_peer(k) * slots + s]

    def source_key(k, s):
        return asked_ref[peer(k), 0, me * slots + s]

    def source_key_far(k, s):
        return asked_ref[far_peer(k), 0, me * slots + s]

    def forward(t, c, host):
        owners = [(peer if host else far_peer)(t * GROUP + u) for u in range(GROUP)]
        here = (t == 0) if host else is_gate & (t * GROUP % inner == 0)
        sem = rad_sem.at[t if host else groups + t]

        @pl.when(here)
        def _():
            settle(fetched_ref, (GROUP - 1) * slots, sem)

        @pl.when(jnp.logical_not(here))
        def _():
            settle(fetched_ref, GROUP * slots, sem)

        got = []
        for p in owners:
            for s in range(slots):
                l = p * slots + s
                form = form_ref[block_ref[0, l]]
                seen = lax.dot_general(
                    fetched_ref[l], form, (((1,), (1,)), ((), ())), preferred_element_type=F32
                )
                got.append(seen * live_of(p, s))
        first = ((0 if host else half) + t * GROUP) * slots
        for i, term in enumerate(got):
            gath_ref[first + i] = term + summed(gath_ref, 0, first + i)
        return c

    gath_ref[links] = jnp.zeros(gath_ref.shape[1:], F32)
    ret_ref[links] = jnp.zeros(ret_ref.shape[1:], F32)
    by_target = link_chain(target_key, target_key_far, 0)
    by_target.start()

    @pl.when(is_gate)
    def _():
        open_table(planes - 1)
        settle(asked_vmem, planes * (inner - 1), idx_sem.at[2])

    @pl.when(jnp.logical_not(is_gate))
    def _():
        settle(asked_vmem, half, idx_sem.at[2])

    beyond = pl.ds(far, half)
    to_smem = pltpu.make_async_copy(asked_vmem.at[beyond], asked_ref.at[beyond], out_sem.at[2])
    to_smem.start()
    by_target.wait()
    to_smem.wait()
    by_source = link_chain(source_key, source_key_far, 2)
    by_source.start()

    def collect(k, peers, base):
        for s in range(slots):
            i = (base + k) * slots + s
            row = arrived_ref[peers(k) * slots + s]
            ret_ref[i] = row.astype(F32) + summed(ret_ref, 2, i)

    def collect_near(t, c):
        for u in range(GROUP):
            collect(t * GROUP + u, peer, 0)
        return c

    def collect_far(t, c):
        settle(arrived_ref, GROUP * slots, bwd_sem.at[1 + t])
        for u in range(GROUP):
            collect(t * GROUP + u, far_peer, half)
        return c

    def scale(c, carry):
        part_ref[c] = refl_ref[c] / area_ref[pl.ds(c, 1), :]
        return carry

    def far_links(t, c):
        forward(t, c, False)
        return collect_far(t, c)

    for load in loads[6:]:
        load.wait()
    lax.fori_loop(0, clusters, scale, 0, unroll=8)
    lax.fori_loop(0, groups, functools.partial(forward, host=True), 0)
    by_source.wait()
    settle(arrived_ref, (half - 1) * slots, bwd_sem.at[0])
    lax.fori_loop(0, groups, collect_near, 0)
    lax.fori_loop(0, groups, far_links, 0)

    def finish(c, carry):
        gathered, returned = summed(gath_ref, 1, c), summed(ret_ref, 3, c)
        out_ref[c] = em_ref[c] + refl_ref[c] * gathered + part_ref[c] * returned
        return carry

    lax.fori_loop(0, clusters, finish, 0, unroll=8)
    settle(asked_vmem, half, send_sems.at[0])
    settle(bwd_ref, (n - 1) * slots, send_sems.at[1])
    settle(served_ref, (half - 1) * slots, send_sems.at[2])
    settle(rad_ref, share, mirror_sem.at[1])

    @pl.when(is_gate)
    def _():
        settle(asked_vmem, planes * (half - 1), send_sems.at[0])
        settle(served_ref, planes * (half - 1) * slots, send_sems.at[2])


def solution(mesh):
    outer, inner = mesh.shape["gx"], mesh.shape["gy"]
    n = outer * inner

    def shards(
        radiance,
        emission,
        reflectance,
        patch_area,
        form_factor,
        source_index,
        target_index,
        block_index,
        valid_count,
    ):
        clusters, bands, patches = radiance.shape
        links = source_index.shape[1]
        slots = links // n
        tile = (bands, patches)
        hbm = pl.BlockSpec(memory_space=pl.ANY)
        rounds = (n // 2).bit_length() - 2
        return pl.pallas_call(
            functools.partial(exchange, outer, inner),
            out_shape=pltpu.VMEM((clusters,) + tile, F32),
            in_specs=[hbm] * 9,
            out_specs=pl.BlockSpec(memory_space=pltpu.VMEM),
            scratch_shapes=[
                pltpu.SMEM(block_index.shape, jnp.int32),
                pltpu.SMEM(target_index.shape, jnp.int32),
                pltpu.SMEM(valid_count.shape, jnp.int32),
                pltpu.VMEM(source_index.shape, jnp.int32),
                pltpu.VMEM(radiance.shape, BF16),
                pltpu.VMEM(patch_area.shape, F32),
                pltpu.VMEM(form_factor.shape, BF16),
                [pltpu.VMEM((clusters,) + tile, BF16)] * (outer // 2),
                pltpu.VMEM((clusters,) + tile, BF16),
                pltpu.VMEM((links,) + tile, BF16),
                pltpu.VMEM(((1 + outer // 2) * links // 2,) + tile, BF16),
                pltpu.VMEM((links,) + tile, BF16),
                pltpu.VMEM((links,) + tile, BF16),
                pltpu.VMEM((links + 1,) + tile, F32),
                pltpu.VMEM((links + 1,) + tile, F32),
                pltpu.VMEM((clusters,) + tile, F32),
                pltpu.VMEM((clusters,) + tile, F32),
                pltpu.VMEM((clusters,) + tile, F32),
                pltpu.VMEM((n, 1, links), jnp.int32),
                pltpu.SMEM((n, 1, links), jnp.int32),
                pltpu.VMEM((links, patches), jnp.int32),
                pltpu.VMEM((4, 1, links), jnp.int32),
                pltpu.SMEM((4, 1, links), jnp.int32),
                pltpu.SemaphoreType.DMA,
                pltpu.SemaphoreType.DMA((8,)),
                pltpu.SemaphoreType.DMA((3,)),
                pltpu.SemaphoreType.DMA((3,)),
                pltpu.SemaphoreType.REGULAR,
                pltpu.SemaphoreType.REGULAR((rounds,)),
                pltpu.SemaphoreType.DMA((2 + outer // 2,)),
                pltpu.SemaphoreType.DMA((3,)),
                pltpu.SemaphoreType.DMA((1 + n // 2 // GROUP,)),
                pltpu.SemaphoreType.DMA((n // GROUP,)),
            ],
            compiler_params=pltpu.CompilerParams(
                collective_id=0, has_side_effects=True, vmem_limit_bytes=EXCHANGE_MIB * 1024 * 1024
            ),
            name="exchange",
        )(
            block_index,
            target_index,
            valid_count,
            source_index,
            radiance,
            patch_area,
            form_factor,
            emission,
            reflectance,
        )

    spec3 = P(("gx", "gy"), None, None)
    spec2 = P(("gx", "gy"), None)
    return jax.shard_map(
        shards,
        mesh=mesh,
        in_specs=(spec3, spec3, spec3, spec2, spec3, spec2, spec2, spec2, spec2),
        out_specs=spec3,
        check_vma=False,
    )
```

time: 31.2 us -> 29.5 us (0.946)
  the two profiles are of different devices: /device:TPU:11 before, /device:TPU:1 now
where the time goes in v3:
time: 29.5 us; the launch traced here: 29.1 us
  Pallas kernels  28.3 us (96%)
  local copies, waits for them, and re-layouts  0.8 us (3%)
    pallas_call x1, Pallas kernels, shards(): pl.pallas_call(functools.partial(exchange, outer, inner), out_shape=pltpu...  28.3 us
    unnamed x1, local copies, waits for them, and re-layouts  0.8 us

profile of v3, /device:TPU:1, one launch (start us, length us, event | category | flops | bytes accessed | tf_op | source)
XLA Modules:
  0.0 29.1 jit_solution(10789586880308049740)
XLA Ops:
  0.0 28.3 %exchange.1 = f32[64,16,128]{2,1,0:T(8,128)S(1)} custom-call(s32[1,128]{1,0:T(1,128)} %block_hbm.1, s32[1,128]{1,0:T(1,128)} %target_hbm.1, s32[1,32]{1,0:T(1,128)} %count_hbm.1, s32[1,128]{1,0:T(1,128)} %source_hbm.1, bf16[64,16,128]{2,1,0:T(8,128)(2,1)} %rad_hbm.1, f32[64,128]{1,0:T(8,128)} %area_hbm.1, bf16[128,128,128]{2,1,0:T(8,128)(2,1)} %form_hbm.1, ...), custom_call_target="tpu_custom_call" | custom-call | tf_op jit(solution)/shard_map/exchange/pallas_call | solution.py:490
  28.3 0.8 %copy.11 = f32[64,16,128]{2,1,0:T(8,128)} copy(f32[64,16,128]{2,1,0:T(8,128)S(1)} %exchange.1) | data formatting | bytes 1048576

commit v4 on v3

--- a/solution.py
+++ b/solution.py
@@ -187,8 +187,16 @@
                 for i in range(first, end):
                     across(i, j).start()
 
+    def turn(k):
+        return (k + inner) % half
+
     def send_idx(k, c):
-        idx_copy(peer(k), 0).start()
+        k = turn(k)
+
+        @pl.when(k != 0)
+        def _():
+            idx_copy(peer(k), 0).start()
+
         return c
 
     def relay_idx(k, c):
@@ -209,17 +217,9 @@
     asked_vmem[me] = source_ref[...]
     for load in loads[2:6]:
         load.wait()
-    for j in range(bits - 1):
+    for j in range(bits - 2):
         pl.semaphore_wait(round_sem.at[j], 1)
-        if j + 1 < bits - 1:
-            tell(j + 1)
-    lax.fori_loop(1, half, send_idx, 0)
-
-    @pl.when(is_gate)
-    def _():
-        pl.semaphore_signal(ready_sem, inc=1, device_id=coords(gate), device_id_type=MESH)
-
-    send_pieces(pieces // 2, pieces)
+        tell(j + 1)
 
     def weigh(c, carry):
         area = area_ref[pl.ds(c, 1), :]
@@ -252,15 +252,22 @@
         return c
 
     def send_near(k, c):
-        bwd_copy(peer(k), 0).start()
+        k = turn(k)
+
+        @pl.when(k != 0)
+        def _():
+            bwd_copy(peer(k), 0).start()
+
         return c
 
     def send_far(k, c):
-        at = depth * inner + (inner - k % inner) % inner
-        bwd_copy(far_peer(k), 1 + at // GROUP).start()
+        to = jnp.where(k < inner, k, gy + k) % inner
+        at = depth * inner + (gy + inner - to) % inner
+        bwd_copy(far_plane(k // inner) + to, 1 + at // GROUP).start()
         return c
 
     def serve(k, c):
+        k = turn(k)
         p = peer(k)
         for s in range(slots):
             served_ref[k * slots + s] = rad_ref[asked_ref[p, 0, me * slots + s]]
@@ -272,16 +279,18 @@
         return c
 
     def serve_table(k, c, j):
-        p = peer(k)
+        to = (mine - gy + inner + k) % half
         owner = far_plane(j) + gy
         base = (1 + j) * half + k
         for s in range(slots):
-            served_ref[base * slots + s] = tables[j][asked_ref[p, 0, owner * slots + s]]
-
-        @pl.when(k != 0)
+            served_ref[base * slots + s] = tables[j][
+                asked_ref[near + to, 0, owner * slots + s]
+            ]
+
+        @pl.when(to != mine)
         def _():
-            at = j * inner + (inner - k % inner) % inner
-            rad_copy(p, owner, base, groups + at // GROUP).start()
+            at = j * inner + (gy + inner - k % inner) % inner
+            rad_copy(near + to, owner, base, groups + at // GROUP).start()
 
         return c
 
@@ -289,19 +298,23 @@
         settle(rad_ref, clusters, mirror_sem.at[2 + j])
         lax.fori_loop(0, half, functools.partial(serve_table, j=j), 0)
         owner = far_plane(j) + gy
+        base = (1 + j) * half + half - inner + gy
         for s in range(slots):
-            fetched_ref[owner * slots + s] = served_ref[(1 + j) * half * slots + s]
+            fetched_ref[owner * slots + s] = served_ref[base * slots + s]
 
     lax.fori_loop(0, groups, back_near, 0)
-    lax.fori_loop(1, half, send_near, 0)
     for s in range(slots):
         arrived_ref[me * slots + s] = bwd_ref[me * slots + s]
+    pl.semaphore_wait(round_sem.at[bits - 2], 1)
+    lax.fori_loop(0, half, send_idx, 0)
+
+    @pl.when(is_gate)
+    def _():
+        pl.semaphore_signal(ready_sem, inc=1, device_id=coords(gate), device_id_type=MESH)
+
+    send_pieces(pieces // 2, pieces)
+    lax.fori_loop(0, half, send_near, 0)
     lax.fori_loop(0, groups, back_far, 0)
-
-    @pl.when(is_gate)
-    def _():
-        settle(asked_vmem, planes, idx_sem.at[1])
-        lax.fori_loop(1, half, relay_idx, 0)
 
     settle(asked_vmem, half - 1, idx_sem.at[0])
     side = pl.ds(near, half)
@@ -314,6 +327,11 @@
 
     @pl.when(is_gate)
     def _():
+        settle(asked_vmem, planes, idx_sem.at[1])
+        lax.fori_loop(1, half, relay_idx, 0)
+
+    @pl.when(is_gate)
+    def _():
         for j in range(planes - 1):
             open_table(j)
 
@@ -326,6 +344,7 @@
             p = near + (mine + j * inner) % half
             pl.semaphore_signal(ready_sem, inc=1, device_id=coords(p), device_id_type=MESH)
 
+    settle(rad_ref, share, mirror_sem.at[1])
     lax.fori_loop(0, half, send_far, 0)
 
     def link_chain(near_key, far_key, row):
@@ -458,7 +477,6 @@
     settle(asked_vmem, half, send_sems.at[0])
     settle(bwd_ref, (n - 1) * slots, send_sems.at[1])
     settle(served_ref, (half - 1) * slots, send_sems.at[2])
-    settle(rad_ref, share, mirror_sem.at[1])
 
     @pl.when(is_gate)
     def _():

time: 29.5 us -> 29.4 us (level)
  the two profiles are of different devices: /device:TPU:1 before, /device:TPU:9 now
where the time goes in v4:
time: 29.4 us; the launch traced here: 29.3 us
  Pallas kernels  28.4 us (97%)
  local copies, waits for them, and re-layouts  0.8 us (3%)
    pallas_call x1, Pallas kernels, shards(): pl.pallas_call(functools.partial(exchange, outer, inner), out_shape=pltpu...  28.4 us
    unnamed x1, local copies, waits for them, and re-layouts  0.8 us

profile of v4, /device:TPU:9, one launch (start us, length us, event | category | flops | bytes accessed | tf_op | source)
XLA Modules:
  0.0 29.3 jit_solution(7879825753295914288)
XLA Ops:
  0.0 28.4 %exchange.1 = f32[64,16,128]{2,1,0:T(8,128)S(1)} custom-call(s32[1,128]{1,0:T(1,128)} %block_hbm.1, s32[1,128]{1,0:T(1,128)} %target_hbm.1, s32[1,32]{1,0:T(1,128)} %count_hbm.1, s32[1,128]{1,0:T(1,128)} %source_hbm.1, bf16[64,16,128]{2,1,0:T(8,128)(2,1)} %rad_hbm.1, f32[64,128]{1,0:T(8,128)} %area_hbm.1, bf16[128,128,128]{2,1,0:T(8,128)(2,1)} %form_hbm.1, ...), custom_call_target="tpu_custom_call" | custom-call | tf_op jit(solution)/shard_map/exchange/pallas_call | solution.py:508
  28.5 0.8 %copy.11 = f32[64,16,128]{2,1,0:T(8,128)} copy(f32[64,16,128]{2,1,0:T(8,128)S(1)} %exchange.1) | data formatting | bytes 1048576

commit v5 on v4

--- a/solution.py
+++ b/solution.py
@@ -9,6 +9,7 @@
 
 MESH = pl.DeviceIdType.MESH
 GROUP = 4
+CORES = 2
 EXCHANGE_MIB = 60
 F32 = jnp.float32
 BF16 = jnp.bfloat16
@@ -37,6 +38,8 @@
     tables,
     weighted_ref,
     bwd_ref,
+    relay_ref,
+    turned_ref,
     served_ref,
     fetched_ref,
     arrived_ref,
@@ -260,11 +263,35 @@
 
         return c
 
-    def send_far(k, c):
-        to = jnp.where(k < inner, k, gy + k) % inner
-        at = depth * inner + (gy + inner - to) % inner
-        bwd_copy(far_plane(k // inner) + to, 1 + at // GROUP).start()
-        return c
+    pair = gy // CORES * CORES
+    my_depth = CORES - 1 - gy % CORES
+
+    def turn_far(k, c):
+        to = (gy + k) % inner
+        host = to // CORES * CORES + CORES - 1 - k // inner
+
+        @pl.when(host != gy)
+        def _():
+            pltpu.make_async_remote_copy(
+                src_ref=bwd_ref.at[pl.ds((far_plane(k // inner) + to) * slots, slots)],
+                dst_ref=relay_ref.at[to % CORES, pl.ds(gy * slots, slots)],
+                send_sem=send_sems.at[1],
+                recv_sem=bwd_sem.at[1],
+                device_id=(gx, host),
+                device_id_type=MESH,
+            ).start()
+
+        return c
+
+    def far_copy(core):
+        return pltpu.make_async_remote_copy(
+            src_ref=relay_ref.at[core],
+            dst_ref=arrived_ref.at[pl.ds(gx * inner * slots, inner * slots)],
+            send_sem=send_sems.at[3],
+            recv_sem=bwd_sem.at[2 + depth],
+            device_id=coords(far_plane(my_depth) + pair + core),
+            device_id_type=MESH,
+        )
 
     def serve(k, c):
         k = turn(k)
@@ -274,7 +301,7 @@
 
         @pl.when(k != 0)
         def _():
-            rad_copy(p, me, k, (half - k) % half // GROUP).start()
+            rad_copy(p, me, k, 0).start()
 
         return c
 
@@ -289,8 +316,7 @@
 
         @pl.when(to != mine)
         def _():
-            at = j * inner + (gy + inner - k % inner) % inner
-            rad_copy(near + to, owner, base, groups + at // GROUP).start()
+            rad_copy(near + to, owner, base, 1 + j).start()
 
         return c
 
@@ -302,19 +328,24 @@
         for s in range(slots):
             fetched_ref[owner * slots + s] = served_ref[base * slots + s]
 
+    lax.fori_loop(0, groups, back_far, 0)
+    for core in range(CORES):
+        for s in range(slots):
+            row = (far_plane(my_depth) + pair + core) * slots + s
+            relay_ref[core, gy * slots + s] = bwd_ref[row]
+    pl.semaphore_wait(round_sem.at[bits - 2], 1)
+    lax.fori_loop(0, half, send_idx, 0)
+
+    @pl.when(is_gate)
+    def _():
+        pl.semaphore_signal(ready_sem, inc=1, device_id=coords(gate), device_id_type=MESH)
+
+    send_pieces(pieces // 2, pieces)
+    lax.fori_loop(0, planes * inner, turn_far, 0)
     lax.fori_loop(0, groups, back_near, 0)
+    lax.fori_loop(0, half, send_near, 0)
     for s in range(slots):
         arrived_ref[me * slots + s] = bwd_ref[me * slots + s]
-    pl.semaphore_wait(round_sem.at[bits - 2], 1)
-    lax.fori_loop(0, half, send_idx, 0)
-
-    @pl.when(is_gate)
-    def _():
-        pl.semaphore_signal(ready_sem, inc=1, device_id=coords(gate), device_id_type=MESH)
-
-    send_pieces(pieces // 2, pieces)
-    lax.fori_loop(0, half, send_near, 0)
-    lax.fori_loop(0, groups, back_far, 0)
 
     settle(asked_vmem, half - 1, idx_sem.at[0])
     side = pl.ds(near, half)
@@ -335,17 +366,29 @@
         for j in range(planes - 1):
             open_table(j)
 
+    last_core = gy % CORES == CORES - 1
+
+    def let_outer(core):
+        for j in range(1, planes):
+            p = near + (mine - gy + j * inner) % half + pair + core
+            pl.semaphore_signal(ready_sem, inc=1, device_id=coords(p), device_id_type=MESH)
+
     settle(rad_ref, clusters - share, mirror_sem.at[0])
     pl.semaphore_wait(ready_sem, 1)
 
-    @pl.when(is_gate)
-    def _():
-        for j in range(1, planes):
-            p = near + (mine + j * inner) % half
-            pl.semaphore_signal(ready_sem, inc=1, device_id=coords(p), device_id_type=MESH)
+    @pl.when(is_gate & last_core)
+    def _():
+        let_outer(CORES - 1)
+
+    @pl.when(is_gate & last_core & (near == 0))
+    def _():
+        for core in range(CORES - 1):
+            let_outer(core)
 
     settle(rad_ref, share, mirror_sem.at[1])
-    lax.fori_loop(0, half, send_far, 0)
+    settle(bwd_ref, planes * (inner - 1) * slots, bwd_sem.at[1])
+    for core in range(CORES):
+        far_copy(core).start()
 
     def link_chain(near_key, far_key, row):
         def fill(k, c, key, base):
@@ -387,27 +430,19 @@
 
     def forward(t, c, host):
         owners = [(peer if host else far_peer)(t * GROUP + u) for u in range(GROUP)]
-        here = (t == 0) if host else is_gate & (t * GROUP % inner == 0)
-        sem = rad_sem.at[t if host else groups + t]
-
-        @pl.when(here)
-        def _():
-            settle(fetched_ref, (GROUP - 1) * slots, sem)
-
-        @pl.when(jnp.logical_not(here))
-        def _():
-            settle(fetched_ref, GROUP * slots, sem)
-
         got = []
-        for p in owners:
-            for s in range(slots):
-                l = p * slots + s
+        first = ((0 if host else half) + t * GROUP) * slots
+        for i, (p, s) in enumerate((p, s) for p in owners for s in range(slots)):
+            l = p * slots + s
+            if host:
                 form = form_ref[block_ref[0, l]]
                 seen = lax.dot_general(
                     fetched_ref[l], form, (((1,), (1,)), ((), ())), preferred_element_type=F32
                 )
-                got.append(seen * live_of(p, s))
-        first = ((0 if host else half) + t * GROUP) * slots
+            else:
+                form = turned_ref[t * GROUP * slots + i]
+                seen = jnp.dot(fetched_ref[l], form, preferred_element_type=F32)
+            got.append(seen * live_of(p, s))
         for i, term in enumerate(got):
             gath_ref[first + i] = term + summed(gath_ref, 0, first + i)
         return c
@@ -446,36 +481,91 @@
         return c
 
     def collect_far(t, c):
-        settle(arrived_ref, GROUP * slots, bwd_sem.at[1 + t])
         for u in range(GROUP):
             collect(t * GROUP + u, far_peer, half)
         return c
+
+    def await_served(j):
+        @pl.when(is_gate)
+        def _():
+            settle(fetched_ref, (inner - 1) * slots, rad_sem.at[1 + j])
+
+        @pl.when(jnp.logical_not(is_gate))
+        def _():
+            settle(fetched_ref, inner * slots, rad_sem.at[1 + j])
 
     def scale(c, carry):
         part_ref[c] = refl_ref[c] / area_ref[pl.ds(c, 1), :]
         return carry
 
-    def far_links(t, c):
-        forward(t, c, False)
-        return collect_far(t, c)
-
     for load in loads[6:]:
         load.wait()
     lax.fori_loop(0, clusters, scale, 0, unroll=8)
+
+    @pl.when(is_gate & last_core & (near != 0))
+    def _():
+        for core in range(CORES - 1):
+            let_outer(core)
+
+    settle(fetched_ref, (half - 1) * slots, rad_sem.at[0])
     lax.fori_loop(0, groups, functools.partial(forward, host=True), 0)
     by_source.wait()
     settle(arrived_ref, (half - 1) * slots, bwd_sem.at[0])
     lax.fori_loop(0, groups, collect_near, 0)
-    lax.fori_loop(0, groups, far_links, 0)
-
-    def finish(c, carry):
-        gathered, returned = summed(gath_ref, 1, c), summed(ret_ref, 3, c)
-        out_ref[c] = em_ref[c] + refl_ref[c] * gathered + part_ref[c] * returned
+
+    def turn_block(t, c):
+        for u in range(GROUP):
+            for s in range(slots):
+                k = t * GROUP + u
+                form = form_ref[block_ref[0, far_peer(k) * slots + s]]
+                turned_ref[k * slots + s] = form.T
+        return c
+
+    lax.fori_loop(0, groups, turn_block, 0)
+    each = inner // GROUP
+
+    def add_forward(j):
+        await_served(j)
+        lax.fori_loop(j * each, (j + 1) * each, functools.partial(forward, host=False), 0)
+
+    def add_backward(j):
+        settle(arrived_ref, inner * slots, bwd_sem.at[2 + j])
+        lax.fori_loop(j * each, (j + 1) * each, collect_far, 0)
+
+    def with_gathered(c, carry, to_ref):
+        to_ref[c] = em_ref[c] + refl_ref[c] * summed(gath_ref, 1, c)
         return carry
 
-    lax.fori_loop(0, clusters, finish, 0, unroll=8)
+    def with_returned(c, carry, to_ref):
+        to_ref[c] = em_ref[c] + part_ref[c] * summed(ret_ref, 3, c)
+        return carry
+
+    def blend(step, to_ref):
+        lax.fori_loop(0, clusters, functools.partial(step, to_ref=to_ref), 0, unroll=8)
+
+    for j in range(planes - 1):
+        add_forward(j)
+        add_backward(j)
+
+    forward_first = is_gate | last_core
+
+    @pl.when(forward_first)
+    def _():
+        add_forward(planes - 1)
+        blend(with_gathered, em_ref)
+        add_backward(planes - 1)
+        blend(with_returned, out_ref)
+
+    @pl.when(jnp.logical_not(forward_first))
+    def _():
+        add_backward(planes - 1)
+        blend(with_returned, em_ref)
+        add_forward(planes - 1)
+        blend(with_gathered, out_ref)
+
     settle(asked_vmem, half, send_sems.at[0])
-    settle(bwd_ref, (n - 1) * slots, send_sems.at[1])
+    settle(bwd_ref, (half - 1 + planes * (inner - 1)) * slots, send_sems.at[1])
+    settle(bwd_ref, half * slots, send_sems.at[3])
     settle(served_ref, (half - 1) * slots, send_sems.at[2])
 
     @pl.when(is_gate)
@@ -521,6 +611,8 @@
                 [pltpu.VMEM((clusters,) + tile, BF16)] * (outer // 2),
                 pltpu.VMEM((clusters,) + tile, BF16),
                 pltpu.VMEM((links,) + tile, BF16),
+                pltpu.VMEM((CORES, inner * slots) + tile, BF16),
+                pltpu.VMEM((links // 2, patches, patches), BF16),
                 pltpu.VMEM(((1 + outer // 2) * links // 2,) + tile, BF16),
                 pltpu.VMEM((links,) + tile, BF16),
                 pltpu.VMEM((links,) + tile, BF16),
@@ -537,13 +629,13 @@
                 pltpu.SemaphoreType.DMA,
                 pltpu.SemaphoreType.DMA((8,)),
                 pltpu.SemaphoreType.DMA((3,)),
-                pltpu.SemaphoreType.DMA((3,)),
+                pltpu.SemaphoreType.DMA((4,)),
                 pltpu.SemaphoreType.REGULAR,
                 pltpu.SemaphoreType.REGULAR((rounds,)),
                 pltpu.SemaphoreType.DMA((2 + outer // 2,)),
                 pltpu.SemaphoreType.DMA((3,)),
-                pltpu.SemaphoreType.DMA((1 + n // 2 // GROUP,)),
-                pltpu.SemaphoreType.DMA((n // GROUP,)),
+                pltpu.SemaphoreType.DMA((2 + outer // 2,)),
+                pltpu.SemaphoreType.DMA((1 + outer // 2,)),
             ],
             compiler_params=pltpu.CompilerParams(
                 collective_id=0, has_side_effects=True, vmem_limit_bytes=EXCHANGE_MIB * 1024 * 1024

time: 29.4 us -> 28.5 us (0.969)
  the two profiles are of different devices: /device:TPU:9 before, /device:TPU:1 now
where the time goes in v5:
time: 28.5 us; the launch traced here: 28.2 us
  Pallas kernels  27.4 us (96%)
  local copies, waits for them, and re-layouts  0.8 us (3%)
    pallas_call x1, Pallas kernels, shards(): pl.pallas_call(functools.partial(exchange, outer, inner), out_shape=pltpu...  27.4 us
    unnamed x1, local copies, waits for them, and re-layouts  0.8 us

profile of v5, /device:TPU:1, one launch (start us, length us, event | category | flops | bytes accessed | tf_op | source)
XLA Modules:
  0.0 28.2 jit_solution(6378633235986893165)
XLA Ops:
  0.0 27.4 %exchange.1 = f32[64,16,128]{2,1,0:T(8,128)S(1)} custom-call(s32[1,128]{1,0:T(1,128)} %block_hbm.1, s32[1,128]{1,0:T(1,128)} %target_hbm.1, s32[1,32]{1,0:T(1,128)} %count_hbm.1, s32[1,128]{1,0:T(1,128)} %source_hbm.1, bf16[64,16,128]{2,1,0:T(8,128)(2,1)} %rad_hbm.1, f32[64,128]{1,0:T(8,128)} %area_hbm.1, bf16[128,128,128]{2,1,0:T(8,128)(2,1)} %form_hbm.1, ...), custom_call_target="tpu_custom_call" | custom-call | tf_op jit(solution)/shard_map/exchange/pallas_call | solution.py:598
  27.4 0.8 %copy.11 = f32[64,16,128]{2,1,0:T(8,128)} copy(f32[64,16,128]{2,1,0:T(8,128)S(1)} %exchange.1) | data formatting | bytes 1048576

commit v6 on v5

--- a/solution.py
+++ b/solution.py
@@ -57,6 +57,7 @@
     in_sem,
     out_sem,
     send_sems,
+    gate_sem,
     ready_sem,
     round_sem,
     mirror_sem,
@@ -74,6 +75,7 @@
     planes = outer // 2
     depth = jnp.where(near == 0, gx, outer - 1 - gx)
     is_gate = depth == planes - 1
+    first_side = near == 0
     gate = jnp.where(near == 0, planes, planes - 1) * inner + gy
     links = block_ref.shape[1]
     slots = links // n
@@ -130,7 +132,11 @@
 
     @pl.when(is_gate)
     def _():
-        for j in range(planes):
+        pl.semaphore_signal(barrier, inc=1, device_id=coords(gate), device_id_type=MESH)
+
+    @pl.when(is_gate & first_side)
+    def _():
+        for j in range(planes - 1):
             pl.semaphore_signal(
                 barrier, inc=1, device_id=coords(far_plane(j) + gy), device_id_type=MESH
             )
@@ -190,6 +196,21 @@
                 for i in range(first, end):
                     across(i, j).start()
 
+    kinds = (
+        (is_gate & first_side, 2),
+        (is_gate & jnp.logical_not(first_side), 2),
+        (jnp.logical_not(is_gate | first_side), 2),
+        (first_side & jnp.logical_not(is_gate), 1),
+    )
+
+    def open_cut(which):
+        kind, count = which
+
+        @pl.when(kind)
+        def _():
+            idx_copy(gate, 1).start()
+            send_pieces(0, count)
+
     def turn(k):
         return (k + inner) % half
 
@@ -213,9 +234,16 @@
 
     for load in loads[:2]:
         load.wait()
-    pl.semaphore_wait(barrier, bits + 1)
-    idx_copy(gate, 1).start()
-    send_pieces(0, pieces // 2)
+    pl.semaphore_wait(barrier, jnp.where(is_gate | (near != 0), bits + 1, bits))
+
+    @pl.when(is_gate & first_side)
+    def _():
+        for j in range(1, planes):
+            p = near + (mine + j * inner) % half
+            pl.semaphore_signal(gate_sem, inc=1, device_id=coords(p), device_id_type=MESH)
+
+    for which in kinds[:3]:
+        open_cut(which)
     tell(0)
     asked_vmem[me] = source_ref[...]
     for load in loads[2:6]:
@@ -223,6 +251,13 @@
     for j in range(bits - 2):
         pl.semaphore_wait(round_sem.at[j], 1)
         tell(j + 1)
+        if j == 0:
+
+            @pl.when(first_side & jnp.logical_not(is_gate))
+            def _():
+                pl.semaphore_wait(gate_sem, 1)
+
+            open_cut(kinds[3])
 
     def weigh(c, carry):
         area = area_ref[pl.ds(c, 1), :]
@@ -340,12 +375,22 @@
     def _():
         pl.semaphore_signal(ready_sem, inc=1, device_id=coords(gate), device_id_type=MESH)
 
-    send_pieces(pieces // 2, pieces)
+    for kind, count in kinds:
+
+        @pl.when(kind)
+        def _():
+            send_pieces(count, pieces)
+
     lax.fori_loop(0, planes * inner, turn_far, 0)
     lax.fori_loop(0, groups, back_near, 0)
     lax.fori_loop(0, half, send_near, 0)
     for s in range(slots):
         arrived_ref[me * slots + s] = bwd_ref[me * slots + s]
+
+    @pl.when(is_gate & jnp.logical_not(first_side))
+    def _():
+        settle(asked_vmem, planes, idx_sem.at[1])
+        lax.fori_loop(1, half, relay_idx, 0)
 
     settle(asked_vmem, half - 1, idx_sem.at[0])
     side = pl.ds(near, half)
@@ -356,7 +401,7 @@
     for s in range(slots):
         fetched_ref[me * slots + s] = served_ref[s]
 
-    @pl.when(is_gate)
+    @pl.when(is_gate & first_side)
     def _():
         settle(asked_vmem, planes, idx_sem.at[1])
         lax.fori_loop(1, half, relay_idx, 0)
@@ -631,6 +676,7 @@
                 pltpu.SemaphoreType.DMA((3,)),
                 pltpu.SemaphoreType.DMA((4,)),
                 pltpu.SemaphoreType.REGULAR,
+                pltpu.SemaphoreType.REGULAR,
                 pltpu.SemaphoreType.REGULAR((rounds,)),
                 pltpu.SemaphoreType.DMA((2 + outer // 2,)),
                 pltpu.SemaphoreType.DMA((3,)),

time: 28.5 us -> 28.1 us (0.986)
  no operation moved by 1% of the time
where the time goes in v6:
time: 28.1 us; the launch traced here: 28 us
  Pallas kernels  27.2 us (97%)
  local copies, waits for them, and re-layouts  0.8 us (3%)
    pallas_call x1, Pallas kernels, shards(): pl.pallas_call(functools.partial(exchange, outer, inner), out_shape=pltpu...  27.2 us
    unnamed x1, local copies, waits for them, and re-layouts  0.8 us

profile of v6, /device:TPU:1, one launch (start us, length us, event | category | flops | bytes accessed | tf_op | source)
XLA Modules:
  0.0 28.0 jit_solution(413158496978802456)
XLA Ops:
  0.0 27.2 %exchange.1 = f32[64,16,128]{2,1,0:T(8,128)S(1)} custom-call(s32[1,128]{1,0:T(1,128)} %block_hbm.1, s32[1,128]{1,0:T(1,128)} %target_hbm.1, s32[1,32]{1,0:T(1,128)} %count_hbm.1, s32[1,128]{1,0:T(1,128)} %source_hbm.1, bf16[64,16,128]{2,1,0:T(8,128)(2,1)} %rad_hbm.1, f32[64,128]{1,0:T(8,128)} %area_hbm.1, bf16[128,128,128]{2,1,0:T(8,128)(2,1)} %form_hbm.1, ...), custom_call_target="tpu_custom_call" | custom-call | tf_op jit(solution)/shard_map/exchange/pallas_call | solution.py:643
  27.2 0.8 %copy.11 = f32[64,16,128]{2,1,0:T(8,128)} copy(f32[64,16,128]{2,1,0:T(8,128)S(1)} %exchange.1) | data formatting | bytes 1048576

commit v7 on v6

--- a/solution.py
+++ b/solution.py
@@ -76,6 +76,8 @@
     depth = jnp.where(near == 0, gx, outer - 1 - gx)
     is_gate = depth == planes - 1
     first_side = near == 0
+    second_gate = is_gate & jnp.logical_not(first_side)
+    second_outer = jnp.logical_not(is_gate | first_side)
     gate = jnp.where(near == 0, planes, planes - 1) * inner + gy
     links = block_ref.shape[1]
     slots = links // n
@@ -99,17 +101,15 @@
 
     loads = [
         pltpu.make_async_copy(src, dst, in_sem.at[i])
-        for i, (src, dst) in enumerate(
-            (
-                (rad_hbm, rad_ref),
-                (source_hbm, source_ref),
-                (area_hbm, area_ref),
-                (block_hbm, block_ref),
-                (target_hbm, target_ref),
-                (count_hbm, count_ref),
-                (em_hbm, em_ref),
-                (refl_hbm, refl_ref),
-            )
+        for src, dst, i in (
+            (rad_hbm, rad_ref, 0),
+            (source_hbm, source_ref, 1),
+            (area_hbm, area_ref, 2),
+            (block_hbm, block_ref, 3),
+            (target_hbm, target_ref, 4),
+            (count_hbm, count_ref, 5),
+            (em_hbm, em_ref, 6),
+            (refl_hbm, refl_ref, 6),
         )
     ]
     forms = [
@@ -128,7 +128,10 @@
     barrier = pltpu.get_barrier_semaphore()
     bits = half.bit_length() - 1
     for j in range(bits):
-        pl.semaphore_signal(barrier, inc=1, device_id=coords(beside(j)), device_id_type=MESH)
+
+        @pl.when(jnp.logical_not(second_gate if j < bits - 1 else second_outer))
+        def _():
+            pl.semaphore_signal(barrier, inc=1, device_id=coords(beside(j)), device_id_type=MESH)
 
     @pl.when(is_gate)
     def _():
@@ -234,7 +237,8 @@
 
     for load in loads[:2]:
         load.wait()
-    pl.semaphore_wait(barrier, jnp.where(is_gate | (near != 0), bits + 1, bits))
+    greeted = jnp.where(first_side & jnp.logical_not(is_gate), bits, bits + 1)
+    pl.semaphore_wait(barrier, jnp.where(second_gate, 1, greeted))
 
     @pl.when(is_gate & first_side)
     def _():
@@ -244,13 +248,21 @@
 
     for which in kinds[:3]:
         open_cut(which)
-    tell(0)
+
+    @pl.when(jnp.logical_not(second_gate))
+    def _():
+        tell(0)
+
     asked_vmem[me] = source_ref[...]
     for load in loads[2:6]:
         load.wait()
     for j in range(bits - 2):
-        pl.semaphore_wait(round_sem.at[j], 1)
-        tell(j + 1)
+
+        @pl.when(jnp.logical_not(second_gate))
+        def _():
+            pl.semaphore_wait(round_sem.at[j], 1)
+            tell(j + 1)
+
         if j == 0:
 
             @pl.when(first_side & jnp.logical_not(is_gate))
@@ -318,12 +330,13 @@
 
         return c
 
-    def far_copy(core):
+    def far_copy(core, part):
+        count = inner // 2 * slots
         return pltpu.make_async_remote_copy(
-            src_ref=relay_ref.at[core],
-            dst_ref=arrived_ref.at[pl.ds(gx * inner * slots, inner * slots)],
+            src_ref=relay_ref.at[core, pl.ds(part * count, count)],
+            dst_ref=arrived_ref.at[pl.ds(gx * inner * slots + part * count, count)],
             send_sem=send_sems.at[3],
-            recv_sem=bwd_sem.at[2 + depth],
+            recv_sem=bwd_sem.at[2 + 2 * depth + part],
             device_id=coords(far_plane(my_depth) + pair + core),
             device_id_type=MESH,
         )
@@ -351,7 +364,8 @@
 
         @pl.when(to != mine)
         def _():
-            rad_copy(near + to, owner, base, 1 + j).start()
+            at = (gy + inner - k % inner) % inner
+            rad_copy(near + to, owner, base, 1 + 2 * j + at // (inner // 2)).start()
 
         return c
 
@@ -368,7 +382,20 @@
         for s in range(slots):
             row = (far_plane(my_depth) + pair + core) * slots + s
             relay_ref[core, gy * slots + s] = bwd_ref[row]
-    pl.semaphore_wait(round_sem.at[bits - 2], 1)
+
+    @pl.when(second_gate)
+    def _():
+        pl.semaphore_wait(gate_sem, 1)
+
+    @pl.when(jnp.logical_not(second_gate))
+    def _():
+        pl.semaphore_wait(round_sem.at[bits - 2], 1)
+
+    @pl.when(second_outer)
+    def _():
+        p = coords(beside(bits - 1))
+        pl.semaphore_signal(gate_sem, inc=1, device_id=p, device_id_type=MESH)
+
     lax.fori_loop(0, half, send_idx, 0)
 
     @pl.when(is_gate)
@@ -433,7 +460,8 @@
     settle(rad_ref, share, mirror_sem.at[1])
     settle(bwd_ref, planes * (inner - 1) * slots, bwd_sem.at[1])
     for core in range(CORES):
-        far_copy(core).start()
+        for part in range(2):
+            far_copy(core, part).start()
 
     def link_chain(near_key, far_key, row):
         def fill(k, c, key, base):
@@ -467,11 +495,14 @@
     def target_key_far(k, s):
         return target_ref[0, far_peer(k) * slots + s]
 
+    def far_source(k):
+        return far_plane(k // inner) + k % inner
+
     def source_key(k, s):
         return asked_ref[peer(k), 0, me * slots + s]
 
     def source_key_far(k, s):
-        return asked_ref[far_peer(k), 0, me * slots + s]
+        return asked_ref[far_source(k), 0, me * slots + s]
 
     def forward(t, c, host):
         owners = [(peer if host else far_peer)(t * GROUP + u) for u in range(GROUP)]
@@ -527,33 +558,37 @@
 
     def collect_far(t, c):
         for u in range(GROUP):
-            collect(t * GROUP + u, far_peer, half)
-        return c
-
-    def await_served(j):
+            collect(t * GROUP + u, far_source, half)
+        return c
+
+    def await_served(j, part):
+        sem = rad_sem.at[1 + 2 * j + part]
+        count = inner // 2
+
         @pl.when(is_gate)
         def _():
-            settle(fetched_ref, (inner - 1) * slots, rad_sem.at[1 + j])
+            settle(fetched_ref, (count - (part == 0)) * slots, sem)
 
         @pl.when(jnp.logical_not(is_gate))
         def _():
-            settle(fetched_ref, inner * slots, rad_sem.at[1 + j])
+            settle(fetched_ref, count * slots, sem)
 
     def scale(c, carry):
         part_ref[c] = refl_ref[c] / area_ref[pl.ds(c, 1), :]
         return carry
 
-    for load in loads[6:]:
-        load.wait()
+    settle(gath_ref, 2 * clusters, in_sem.at[6])
     lax.fori_loop(0, clusters, scale, 0, unroll=8)
+
+    settle(fetched_ref, (half - 1) * slots, rad_sem.at[0])
+    lax.fori_loop(0, groups // 2, functools.partial(forward, host=True), 0)
 
     @pl.when(is_gate & last_core & (near != 0))
     def _():
         for core in range(CORES - 1):
             let_outer(core)
 
-    settle(fetched_ref, (half - 1) * slots, rad_sem.at[0])
-    lax.fori_loop(0, groups, functools.partial(forward, host=True), 0)
+    lax.fori_loop(groups // 2, groups, functools.partial(forward, host=True), 0)
     by_source.wait()
     settle(arrived_ref, (half - 1) * slots, bwd_sem.at[0])
     lax.fori_loop(0, groups, collect_near, 0)
@@ -570,12 +605,16 @@
     each = inner // GROUP
 
     def add_forward(j):
-        await_served(j)
-        lax.fori_loop(j * each, (j + 1) * each, functools.partial(forward, host=False), 0)
+        for part in range(2):
+            await_served(j, part)
+            first = j * each + part * each // 2
+            lax.fori_loop(first, first + each // 2, functools.partial(forward, host=False), 0)
 
     def add_backward(j):
-        settle(arrived_ref, inner * slots, bwd_sem.at[2 + j])
-        lax.fori_loop(j * each, (j + 1) * each, collect_far, 0)
+        for part in range(2):
+            settle(arrived_ref, inner // 2 * slots, bwd_sem.at[2 + 2 * j + part])
+            first = j * each + part * each // 2
+            lax.fori_loop(first, first + each // 2, collect_far, 0)
 
     def with_gathered(c, carry, to_ref):
         to_ref[c] = em_ref[c] + refl_ref[c] * summed(gath_ref, 1, c)
@@ -592,7 +631,7 @@
         add_forward(j)
         add_backward(j)
 
-    forward_first = is_gate | last_core
+    forward_first = is_gate
 
     @pl.when(forward_first)
     def _():
@@ -672,7 +711,7 @@
                 pltpu.VMEM((4, 1, links), jnp.int32),
                 pltpu.SMEM((4, 1, links), jnp.int32),
                 pltpu.SemaphoreType.DMA,
-                pltpu.SemaphoreType.DMA((8,)),
+                pltpu.SemaphoreType.DMA((7,)),
                 pltpu.SemaphoreType.DMA((3,)),
                 pltpu.SemaphoreType.DMA((4,)),
                 pltpu.SemaphoreType.REGULAR,
@@ -680,8 +719,8 @@
                 pltpu.SemaphoreType.REGULAR((rounds,)),
                 pltpu.SemaphoreType.DMA((2 + outer // 2,)),
                 pltpu.SemaphoreType.DMA((3,)),
-                pltpu.SemaphoreType.DMA((2 + outer // 2,)),
-                pltpu.SemaphoreType.DMA((1 + outer // 2,)),
+                pltpu.SemaphoreType.DMA((2 + outer,)),
+                pltpu.SemaphoreType.DMA((1 + outer,)),
             ],
             compiler_params=pltpu.CompilerParams(
                 collective_id=0, has_side_effects=True, vmem_limit_bytes=EXCHANGE_MIB * 1024 * 1024

time: 28.1 us -> 28 us (level)
  Pallas kernels: 27.2 us -> 26.9 us
where the time goes in v7:
time: 28 us; the launch traced here: 27.7 us
  Pallas kernels  26.9 us (96%)
  local copies, waits for them, and re-layouts  0.8 us (3%)
    pallas_call x1, Pallas kernels, shards(): pl.pallas_call(functools.partial(exchange, outer, inner), out_shape=pltpu...  26.9 us
    unnamed x1, local copies, waits for them, and re-layouts  0.8 us

profile of v7, /device:TPU:1, one launch (start us, length us, event | category | flops | bytes accessed | tf_op | source)
XLA Modules:
  0.0 27.7 jit_solution(7120783023507536130)
XLA Ops:
  0.0 26.9 %exchange.1 = f32[64,16,128]{2,1,0:T(8,128)S(1)} custom-call(s32[1,128]{1,0:T(1,128)} %block_hbm.1, s32[1,128]{1,0:T(1,128)} %target_hbm.1, s32[1,32]{1,0:T(1,128)} %count_hbm.1, s32[1,128]{1,0:T(1,128)} %source_hbm.1, bf16[64,16,128]{2,1,0:T(8,128)(2,1)} %rad_hbm.1, f32[64,128]{1,0:T(8,128)} %area_hbm.1, bf16[128,128,128]{2,1,0:T(8,128)(2,1)} %form_hbm.1, ...), custom_call_target="tpu_custom_call" | custom-call | tf_op jit(solution)/shard_map/exchange/pallas_call | solution.py:682
  26.9 0.8 %copy.11 = f32[64,16,128]{2,1,0:T(8,128)} copy(f32[64,16,128]{2,1,0:T(8,128)S(1)} %exchange.1) | data formatting | bytes 1048576

commit v8 on v7

--- a/solution.py
+++ b/solution.py
@@ -580,15 +580,13 @@
     settle(gath_ref, 2 * clusters, in_sem.at[6])
     lax.fori_loop(0, clusters, scale, 0, unroll=8)
 
-    settle(fetched_ref, (half - 1) * slots, rad_sem.at[0])
-    lax.fori_loop(0, groups // 2, functools.partial(forward, host=True), 0)
-
     @pl.when(is_gate & last_core & (near != 0))
     def _():
         for core in range(CORES - 1):
             let_outer(core)
 
-    lax.fori_loop(groups // 2, groups, functools.partial(forward, host=True), 0)
+    settle(fetched_ref, (half - 1) * slots, rad_sem.at[0])
+    lax.fori_loop(0, groups, functools.partial(forward, host=True), 0)
     by_source.wait()
     settle(arrived_ref, (half - 1) * slots, bwd_sem.at[0])
     lax.fori_loop(0, groups, collect_near, 0)
@@ -631,7 +629,7 @@
         add_forward(j)
         add_backward(j)
 
-    forward_first = is_gate
+    forward_first = is_gate | last_core
 
     @pl.when(forward_first)
     def _():

time: 28 us -> 28 us (level)
  no operation moved by 1% of the time
where the time goes in v8:
time: 28 us; the launch traced here: 27.7 us
  Pallas kernels  26.9 us (96%)
  local copies, waits for them, and re-layouts  0.8 us (3%)
    pallas_call x1, Pallas kernels, shards(): pl.pallas_call(functools.partial(exchange, outer, inner), out_shape=pltpu...  26.9 us
    unnamed x1, local copies, waits for them, and re-layouts  0.8 us

profile of v8, /device:TPU:1, one launch (start us, length us, event | category | flops | bytes accessed | tf_op | source)
XLA Modules:
  0.0 27.7 jit_solution(3185545292609351441)
XLA Ops:
  0.0 26.9 %exchange.1 = f32[64,16,128]{2,1,0:T(8,128)S(1)} custom-call(s32[1,128]{1,0:T(1,128)} %block_hbm.1, s32[1,128]{1,0:T(1,128)} %target_hbm.1, s32[1,32]{1,0:T(1,128)} %count_hbm.1, s32[1,128]{1,0:T(1,128)} %source_hbm.1, bf16[64,16,128]{2,1,0:T(8,128)(2,1)} %rad_hbm.1, f32[64,128]{1,0:T(8,128)} %area_hbm.1, bf16[128,128,128]{2,1,0:T(8,128)(2,1)} %form_hbm.1, ...), custom_call_target="tpu_custom_call" | custom-call | tf_op jit(solution)/shard_map/exchange/pallas_call | solution.py:680
  26.9 0.8 %copy.11 = f32[64,16,128]{2,1,0:T(8,128)} copy(f32[64,16,128]{2,1,0:T(8,128)S(1)} %exchange.1) | data formatting | bytes 1048576
